TPU v7x, 256 devices: a whole 4x4x8 slice. The times are simulated.
256 devices in a mesh: ord: 16 (over x, z_hi, core), blk: 16 (over z_lo, y).
Axes of the slice: x: 4, y: 4, z: 8 (z_hi: 2, z_lo: 4; z = z_hi * 4 + z_lo), core: 2. Of those that a mesh axis runs over, the one named last changes fastest.
Arguments:
- coefficients: bfloat16 [128, 2, 256, 8192], P('ord', None, None, 'blk'), may hold values from -0.52734375 to 0.52734375
- leaf_factors: bfloat16 [128, 128, 8192], P('ord', None, 'blk'), may hold values from -0.25 to 0.25
- level_interpolants: bfloat16 [3, 2, 128, 128, 2048], P(None, None, 'ord', None, 'blk'), may hold values from -0.375 to 0.375
- latitude_factors: bfloat16 [128, 10240, 128], P('ord', 'blk'), may hold values from -0.5 to 0.5
- order_ids: int32 [128], replicated, may hold values from 0 to 8191, as said below
Outputs:
- products: bfloat16 [256, 128, 10240], P(None, 'ord', 'blk')
Inputs may be any that keep to these rules, and one draw needn't show every extreme that they name: `order_ids`: the slots hold distinct orders of the truncation.
All inputs are finite; a program needn't handle non-finite values.
Results may differ from a plain program's by a relative error of at most 0.011.
Values may be sent and summed in bfloat16 or wider, within the bound.
No kernel may reach another device: no remote copies, remote signals or barrier semaphores. Data moves between devices by JAX's collectives and lax.ppermute only.
A program may use at most 64 MiB of HBM per device.

v0:
```python
import math

import jax
import jax.numpy as jnp
from jax import lax
from jax.sharding import PartitionSpec as P

PERIOD = 16384
NLON = 256


def partner(shard, axis, apart):
    return lax.ppermute(shard, axis, [(i, i ^ 1 << apart) for i in range(lax.axis_size(axis))])


def synthesis_table(order_ids, count, period):
    steps = jnp.arange(count, dtype=jnp.int32)
    phase = (order_ids[:, None] * steps[None, :] % period).astype(jnp.float32) * (
        2.0 * math.pi / period
    )
    weight = jnp.where(order_ids == 0, 1.0, 2.0).astype(jnp.float32)[:, None]
    table = jnp.stack([weight * jnp.cos(phase), -weight * jnp.sin(phase)], axis=1)
    return table.astype(jnp.bfloat16)


def per_device(coefficients, leaf_factors, level_interpolants, latitude_factors, order_ids):
    orders_here, parts, fields, leaf = coefficients.shape
    flat = coefficients.reshape(orders_here, parts * fields, leaf)
    combined_sum = jnp.einsum(
        "mcl,mrl->mcr", flat, leaf_factors, preferred_element_type=jnp.float32
    ).astype(jnp.bfloat16)
    level_count = level_interpolants.shape[0]
    top_bit = lax.axis_size("blk").bit_length() - 1
    for tree_level in range(level_count):
        partner_block = partner(combined_sum, "blk", top_bit - 1 - tree_level)
        mixed = jnp.einsum(
            "dfx,dhx->dfh",
            combined_sum,
            level_interpolants[tree_level, 0],
            preferred_element_type=jnp.float32,
        )
        mixed = mixed + jnp.einsum(
            "dfx,dhx->dfh",
            partner_block,
            level_interpolants[tree_level, 1],
            preferred_element_type=jnp.float32,
        )
        combined_sum = mixed.astype(jnp.bfloat16)
    lat_here = latitude_factors.shape[1]
    values = jnp.einsum(
        "mcr,mlr->mcl", combined_sum, latitude_factors, preferred_element_type=jnp.float32
    )
    values = values.astype(jnp.bfloat16).reshape(orders_here, parts, fields, lat_here)
    regrouped = lax.all_to_all(values, "ord", split_axis=2, concat_axis=0, tiled=True)
    total_orders, parts_again, group, lat_count = regrouped.shape
    table = synthesis_table(order_ids, NLON, PERIOD).reshape(total_orders * parts_again, NLON)
    stacked_blocks = regrouped.reshape(total_orders * parts_again, group * lat_count)
    grid = lax.dot_general(
        table, stacked_blocks, (((0,), (0,)), ((), ())), preferred_element_type=jnp.float32
    )
    grid = grid.reshape(NLON, group // 2, 2, lat_count)
    return (grid[:, :, 0, :] * grid[:, :, 1, :]).astype(jnp.bfloat16)


def solution(mesh):
    in_specs = (
        P("ord", None, None, "blk"),
        P("ord", None, "blk"),
        P(None, None, "ord", None, "blk"),
        P("ord", "blk", None),
        P(),
    )
    out_specs = P(None, "ord", "blk")
    return jax.shard_map(
        per_device, mesh=mesh, in_specs=in_specs, out_specs=out_specs, check_vma=False
    )
```

profile of v0, /device:TPU:72, one launch (start us, length us, event | category | flops | bytes accessed | tf_op | source)
XLA Modules:
  0.0 277.4 jit_solution(16014737381392004320)
XLA Ops:
  0.0 0.0 copy-start
  0.0 0.0 copy-start.2
  0.0 3.9 %convolution_convert_fusion.1 = bf16[8,512,128]{2,1,0:T(8,128)(2,1)S(1)} fusion(bf16[8,512,512]{2,1,0:T(8,128)(2,1)} %bitcast.50, bf16[8,128,512]{2,1,0:T(8,128)(2,1)} %param.6), kind=kOutput, calls=%fused_computation.7 | convolution fusion | flops 537395200 | bytes 6291456 | tf_op jit(solution)/shard_map/mcl,mrl->mcr/dot_general | solution.py:29
  3.9 0.1 collective-permute-start
  4.0 0.0 copy-done.2
  4.0 0.4 fusion.10
  4.4 44.7 %collective-permute-done = bf16[8,512,128]{2,1,0:T(8,128)(2,1)S(1)} collective-permute-done((bf16[8,512,128]{2,1,0:T(8,128)(2,1)S(1)}, bf16[8,512,128]{2,1,0:T(8,128)(2,1)S(1)}, u32[]{:S(2)}, u32[]{:S(2)}) %collective-permute-start) | collective-permute-done | bytes 1048608 | tf_op jit(solution)/shard_map/ppermute | solution.py:13
  49.2 0.4 add_convert_fusion.2
  49.6 4.6 %collective-permute-start.1 = (bf16[8,512,128]{2,1,0:T(8,128)(2,1)S(1)}, bf16[8,512,128]{2,1,0:T(8,128)(2,1)S(1)}, u32[]{:S(2)}, u32[]{:S(2)}) collective-permute-start(bf16[8,512,128]{2,1,0:T(8,128)(2,1)S(1)} %add_convert_fusion.2), channel_id=1, source_target_pairs={{0,4},{1,5},{2,6},{3,7},{4,0},{5,1},{6,2},{7,3},{8,12},{9,13},{10,... | collective-permute-start | bytes 3145736 | tf_op jit(solution)/shard_map/ppermute | solution.py:13
  54.2 0.4 fusion.7
  54.7 22.9 %collective-permute-done.1 = bf16[8,512,128]{2,1,0:T(8,128)(2,1)S(1)} collective-permute-done((bf16[8,512,128]{2,1,0:T(8,128)(2,1)S(1)}, bf16[8,512,128]{2,1,0:T(8,128)(2,1)S(1)}, u32[]{:S(2)}, u32[]{:S(2)}) %collective-permute-start.1) | collective-permute-done | bytes 1048608 | tf_op jit(solution)/shard_map/ppermute | solution.py:13
  77.6 0.4 add_convert_fusion.1
  78.0 2.4 collective-permute-start.2
  80.4 0.4 fusion.4
  80.9 23.4 %collective-permute-done.2 = bf16[8,512,128]{2,1,0:T(8,128)(2,1)} collective-permute-done((bf16[8,512,128]{2,1,0:T(8,128)(2,1)S(1)}, bf16[8,512,128]{2,1,0:T(8,128)(2,1)}, u32[]{:S(2)}, u32[]{:S(2)}) %collective-permute-start.2) | collective-permute-done | bytes 1048608 | tf_op jit(solution)/shard_map/ppermute | solution.py:13
  104.2 0.0 copy-done
  104.2 5.4 %convolution_convert_fusion = bf16[8,512,640]{2,1,0:T(8,128)(2,1)} fusion(bf16[8,640,128]{2,1,0:T(8,128)(2,1)S(1)} %copy-done, f32[8,512,128]{2,1,0:T(8,128)S(1)} %fusion.4, bf16[8,512,128]{2,1,0:T(8,128)(2,1)} %collective-permute-done.2, bf16[3,2,8,128,128]{4,3,2,1,0:T(8,128)(2,1)} %param.7), kind=kOutput, calls=%fused_computation.2 | convolution fusion | flops 808976384 | bytes 9961472 | tf_op jit(solution)/shard_map/mcr,mlr->mcl/dot_general | solution.py:50
  109.6 10.2 %copy.22 = bf16[8,2,256,640]{3,1,0,2:T(2,128)(2,1)} copy(bf16[8,2,256,640]{3,2,1,0:T(8,128)(2,1)} %bitcast.45) | data formatting | bytes 10485760 | tf_op jit(solution)/shard_map/reshape | solution.py:53
  119.8 0.0 copy-start.3
  119.8 8.3 %all-to-all-start = ((bf16[8,2,256,640]{3,1,0,2:T(2,128)(2,1)}), bf16[8,2,256,640]{3,1,0,2:T(2,128)(2,1)}, u32[]{:S(2)}, u32[]{:S(2)}) async-start(bf16[8,2,256,640]{3,1,0,2:T(2,128)(2,1)} %copy.22), calls=%async_computation | async-start | bytes 10485760 | tf_op jit(solution)/shard_map/all_to_all | solution.py:54
  128.1 0.0 copy-done.3
  128.1 0.6 multiply_convert_fusion.1
  128.7 0.1 copy.21
  128.9 0.1 convert_element_type.47
  128.9 124.6 %all-to-all-done = bf16[8,2,256,640]{3,1,0,2:T(2,128)(2,1)} async-done(((bf16[8,2,256,640]{3,1,0,2:T(2,128)(2,1)}), bf16[8,2,256,640]{3,1,0,2:T(2,128)(2,1)}, u32[]{:S(2)}, u32[]{:S(2)}) %all-to-all-start) | async-done | bytes 5242912 | tf_op jit(solution)/shard_map/all_to_all | solution.py:54
  253.5 3.7 %copy.23 = bf16[8,2,256,640]{3,2,1,0:T(8,128)(2,1)S(1)} copy(bf16[8,2,256,640]{3,1,0,2:T(2,128)(2,1)} %all-to-all-done) | data formatting | bytes 10485760 | tf_op jit(solution)/shard_map/all_to_all | solution.py:54
  257.2 0.7 copy.24
  258.0 3.9 %copy.30 = bf16[32,8,16,640]{3,1,2,0:T(8,128)(2,1)} copy(bf16[32,8,16,640]{3,2,1,0:T(8,128)(2,1)S(1)} %bitcast.48) | data formatting | bytes 10485760
  261.8 7.9 %copy.25 = bf16[10240,256]{1,0:T(8,128)(2,1)} copy(bf16[10240,256]{0,1:T(8,128)(2,1)} %bitcast.49) | data formatting | bytes 10485760 | tf_op jit(solution)/shard_map/dot_general | solution.py:58
  269.7 4.1 %fusion.22 = f32[256,8,2,640]{3,0,2,1:T(8,128)S(1)} fusion(bf16[8,2,640,256]{3,2,1,0:T(8,128)(2,1)} %bitcast.46, bf16[256,256]{1,0:T(8,128)(2,1)S(1)} %convert_element_type.47), kind=kOutput, calls=%fused_computation.30 | convolution fusion | flops 1342177280 | bytes 15859712 | tf_op jit(solution)/shard_map/dot_general | solution.py:58
  273.8 0.0 copy-start.1
  273.8 0.6 fusion.1
  274.4 3.0 %copy.27 = bf16[256,8,640]{2,1,0:T(8,128)(2,1)} copy(bf16[256,8,640]{2,0,1:T(8,128)(2,1)S(1)} %fusion.1) | data formatting | bytes 5242880 | tf_op jit(solution)/shard_map/convert_element_type | solution.py:62
  277.4 0.0 copy-done.1
  (2 shorter events, 0.0 us)
Async XLA Ops:
  0.0 104.2 %copy-start = (bf16[8,640,128]{2,1,0:T(8,128)(2,1)S(1)}, bf16[8,640,128]{2,1,0:T(8,128)(2,1)}, u32[]{:S(2)}) copy-start(bf16[8,640,128]{2,1,0:T(8,128)(2,1)} %param.8) | copy-start | bytes 3932164
  0.0 4.0 %copy-start.2 = (bf16[3,2,8,128,128]{4,3,2,1,0:T(8,128)(2,1)S(1)}, bf16[3,2,8,128,128]{4,3,2,1,0:T(8,128)(2,1)}, u32[]{:S(2)}) copy-start(bf16[3,2,8,128,128]{4,3,2,1,0:T(8,128)(2,1)} %param.7) | copy-start | bytes 4718596
  3.9 45.3 %collective-permute-start = (bf16[8,512,128]{2,1,0:T(8,128)(2,1)S(1)}, bf16[8,512,128]{2,1,0:T(8,128)(2,1)S(1)}, u32[]{:S(2)}, u32[]{:S(2)}) collective-permute-start(bf16[8,512,128]{2,1,0:T(8,128)(2,1)S(1)} %convolution_convert_fusion.1), channel_id=1, source_target_pairs={{0,8},{1,9},{2,10},{3,11},{4,12},{5,13},{6,14},{7,15},{8,0},{9,1},... | collective-permute-start | bytes 3145736 | tf_op jit(solution)/shard_map/ppermute | solution.py:13
  49.6 28.0 %collective-permute-start.1 = (bf16[8,512,128]{2,1,0:T(8,128)(2,1)S(1)}, bf16[8,512,128]{2,1,0:T(8,128)(2,1)S(1)}, u32[]{:S(2)}, u32[]{:S(2)}) collective-permute-start(bf16[8,512,128]{2,1,0:T(8,128)(2,1)S(1)} %add_convert_fusion.2), channel_id=1, source_target_pairs={{0,4},{1,5},{2,6},{3,7},{4,0},{5,1},{6,2},{7,3},{8,12},{9,13},{10,... | collective-permute-start | bytes 3145736 | tf_op jit(solution)/shard_map/ppermute | solution.py:13
  78.0 26.2 %collective-permute-start.2 = (bf16[8,512,128]{2,1,0:T(8,128)(2,1)S(1)}, bf16[8,512,128]{2,1,0:T(8,128)(2,1)}, u32[]{:S(2)}, u32[]{:S(2)}) collective-permute-start(bf16[8,512,128]{2,1,0:T(8,128)(2,1)S(1)} %add_convert_fusion.1), channel_id=1, source_target_pairs={{0,2},{1,3},{2,0},{3,1},{4,6},{5,7},{6,4},{7,5},{8,10},{9,11},{10,... | collective-permute-start | bytes 3145736 | tf_op jit(solution)/shard_map/ppermute | solution.py:13
  119.8 8.3 %copy-start.3 = (s32[128]{0:T(128)S(1)}, s32[128]{0:T(128)}, u32[]{:S(2)}) copy-start(s32[128]{0:T(128)} %param.9) | copy-start | bytes 1540
  119.8 133.7 %all-to-all-start = ((bf16[8,2,256,640]{3,1,0,2:T(2,128)(2,1)}), bf16[8,2,256,640]{3,1,0,2:T(2,128)(2,1)}, u32[]{:S(2)}, u32[]{:S(2)}) async-start(bf16[8,2,256,640]{3,1,0,2:T(2,128)(2,1)} %copy.22), calls=%async_computation | async-start | bytes 10485760 | tf_op jit(solution)/shard_map/all_to_all | solution.py:54
  273.8 3.6 %copy-start.1 = (bf16[8,640,128]{2,1,0:T(8,128)(2,1)S(1)}, bf16[8,640,128]{2,1,0:T(8,128)(2,1)}, u32[]{:S(2)}) copy-start(bf16[8,640,128]{2,1,0:T(8,128)(2,1)} %param.8) | copy-start | bytes 3932164
where the time goes:
time: 278 us; the launch traced here: 277 us
  waiting for transfers between devices  216 us (78%)
  local copies, waits for them, and re-layouts  29.6 us (11%)
  matrix products  15.5 us (6%)
  starting transfers between devices  15.4 us (6%)
    all_to_all x1, waiting for transfers between devices, per_device(): lax.all_to_all(values, 'ord', split_axis=2, concat_axis=0, tiled=True)  125 us
    ppermute x3, waiting for transfers between devices, partner(): lax.ppermute(shard, axis, [(i, i ^ 1 << apart) for i in range(lax.axis_si...  91 us
    reshape x1, local copies, waits for them, and re-layouts, per_device(): values.astype(jnp.bfloat16).reshape(orders_here, parts, fields, lat_here)  10.2 us
    all_to_all x1, starting transfers between devices, per_device(): lax.all_to_all(values, 'ord', split_axis=2, concat_axis=0, tiled=True)  8.26 us
    dot_general x1, local copies, waits for them, and re-layouts, per_device(): lax.dot_general(table, stacked_blocks, (((0,), (0,)), ((), ())), preferre...  7.91 us
    ppermute x3, starting transfers between devices, partner(): lax.ppermute(shard, axis, [(i, i ^ 1 << apart) for i in range(lax.axis_si...  7.12 us
  transfers between devices with their start and end apart: 4, of which 4 were waited for; matrix products, arithmetic and copies ran while one was open for 1% of the time, Pallas kernels for 0%

commit v1 on v0

v1 whole, which is shorter than its diff:
```python
import math

import jax
import jax.numpy as jnp
from jax import lax
from jax.sharding import PartitionSpec as P


PERIOD = 16384
NLON = 256
SPLIT = 384
PIECE = 128


def xor_permute(shard, axis, mask):
    return lax.ppermute(shard, axis, [(i, i ^ mask) for i in range(lax.axis_size(axis))])


def synthesis_table(order_ids, count, period):
    steps = jnp.arange(count, dtype=jnp.int32)
    phase = (order_ids[:, None] * steps[None, :] % period).astype(jnp.float32) * (
        2.0 * math.pi / period
    )
    weight = jnp.where(order_ids == 0, 1.0, 2.0).astype(jnp.float32)[:, None]
    table = jnp.stack([weight * jnp.cos(phase), -weight * jnp.sin(phase)], axis=1)
    return table.astype(jnp.bfloat16)


def per_device(coefficients, leaf_factors, level_interpolants, latitude_factors, order_ids):
    m, parts, fields, leaf = coefficients.shape
    size = lax.axis_size("ord")
    group = fields // size
    half = size // 2
    side = (lax.axis_index("ord") >> 1) & 1
    by_side = coefficients.reshape(m, parts, size // 4, 2, 2 * group, leaf)

    def leaves(which):
        chosen = lax.dynamic_index_in_dim(by_side, which, 3, keepdims=False)
        flat = chosen.reshape(m, parts * half * group, leaf)
        return jnp.einsum(
            "mcl,mrl->mcr", flat, leaf_factors, preferred_element_type=jnp.float32
        ).astype(jnp.bfloat16)

    top = lax.axis_size("blk") // 2

    def level(k, here, there):
        mixed = jnp.einsum(
            "mcx,mhx->mch", here, level_interpolants[k, 0], preferred_element_type=jnp.float32
        ) + jnp.einsum(
            "mcx,mhx->mch", there, level_interpolants[k, 1], preferred_element_type=jnp.float32
        )
        return mixed.astype(jnp.bfloat16)

    near, far = leaves(side), leaves(1 - side)
    crossing = lambda shard: xor_permute(shard, "ord", 2)
    pieces = [
        crossing(latitude_factors[:, i : i + PIECE])
        for i in range(0, latitude_factors.shape[1], PIECE)
    ]
    lat_far = (
        jnp.concatenate(pieces[: SPLIT // PIECE], 1),
        jnp.concatenate(pieces[SPLIT // PIECE :], 1),
    )
    for k in range(level_interpolants.shape[0]):
        near = level(k, near, xor_permute(near, "blk", top >> k))
        far = level(k, far, xor_permute(far, "blk", top >> k))
    crossed = crossing(far)
    groups = [[i for i in range(size) if (i >> 1) & 1 == s] for s in (0, 1)]

    def regroup(reduced, factors):
        values = jnp.einsum(
            "mcr,mlr->mcl", reduced, factors, preferred_element_type=jnp.float32
        ).astype(jnp.bfloat16)
        values = values.reshape(m * parts, half, group, -1)
        values = values.transpose(1, 2, 0, 3)
        return lax.all_to_all(values, "ord", 0, 0, axis_index_groups=groups, tiled=True)

    table = synthesis_table(order_ids, NLON, PERIOD).reshape(size // 4, 2, 2 * m * parts, NLON)

    def rows(which):
        return lax.dynamic_index_in_dim(table, which, 1, keepdims=False).reshape(half, m * parts, NLON)

    def partial_grid(which, values):
        return jnp.einsum("sak,sfal->kfl", rows(which), values, preferred_element_type=jnp.float32)

    base = partial_grid(side, regroup(near, latitude_factors))
    bases = (base[:, :, :SPLIT], base[:, :, SPLIT:])
    outs = []
    for part, factors in zip(bases, lat_far):
        grid = part + partial_grid(1 - side, regroup(crossed, factors))
        grid = grid.reshape(NLON, group // 2, 2, -1)
        outs.append((grid[:, :, 0, :] * grid[:, :, 1, :]).astype(jnp.bfloat16))
    return jnp.concatenate(outs, -1)


def solution(mesh):
    in_specs = (
        P("ord", None, None, "blk"),
        P("ord", None, "blk"),
        P(None, None, "ord", None, "blk"),
        P("ord", "blk", None),
        P(),
    )
    out_specs = P(None, "ord", "blk")

    return jax.shard_map(
        per_device, mesh=mesh, in_specs=in_specs, out_specs=out_specs, check_vma=False
    )
```

time: 278 us -> 242 us (0.87)
  the two profiles are of different devices: /device:TPU:72 before, /device:TPU:1 now
where the time goes in v1:
time: 242 us; the launch traced here: 241 us
  waiting for transfers between devices  139 us (57%)
  starting transfers between devices  56.4 us (23%)
  matrix products  21.7 us (9%)
  local copies, waits for them, and re-layouts  15.8 us (7%)
  other arithmetic  8.51 us (4%)
    ppermute x12, waiting for transfers between devices, xor_permute(): lax.ppermute(shard, axis, [(i, i ^ mask) for i in range(lax.axis_size(axi...  127 us
    ppermute x12, starting transfers between devices, xor_permute(): lax.ppermute(shard, axis, [(i, i ^ mask) for i in range(lax.axis_size(axi...  33.1 us
    all_to_all x3, starting transfers between devices, regroup(): lax.all_to_all(values, 'ord', 0, 0, axis_index_groups=groups, tiled=True)  23.3 us
    all_to_all x3, waiting for transfers between devices, regroup(): lax.all_to_all(values, 'ord', 0, 0, axis_index_groups=groups, tiled=True)  11.6 us
    dot_general x3, matrix products, partial_grid(): jnp.einsum('sak,sfal->kfl', rows(which), values, preferred_element_type=j...  10.3 us
    reshape x3, local copies, waits for them, and re-layouts, regroup(): values = values.reshape(m * parts, half, group, -1)  6.66 us
    convert_element_type x2, other arithmetic, per_device(): outs.append((grid[:, :, 0, :] * grid[:, :, 1, :]).astype(jnp.bfloat16))  6.12 us
  transfers between devices with their start and end apart: 15, of which 10 were waited for; matrix products, arithmetic and copies ran while one was open for 11% of the time, Pallas kernels for 0%

profile of v1, /device:TPU:1, one launch (start us, length us, event | category | flops | bytes accessed | tf_op | source)
XLA Modules:
  0.0 241.2 jit_solution(2886816866806175332)
XLA Ops:
  0.0 2.6 %constant_dynamic-slice_fusion = (bf16[8,2,4,1,32,512]{5,4,3,2,1,0:T(8,128)(2,1)S(1)}, bf16[8,2,4,1,32,512]{5,4,3,2,1,0:T(8,128)(2,1)S(1)}) fusion(bf16[8,2,4,2,32,512]{5,4,3,2,1,0:T(8,128)(2,1)} %bitcast.109, s32[]{:T(128)S(6)} %select_n.36, s32[]{:T(128)S(6)} %select_n.35), kind=kLoop, calls=%fused_computation.81 | loop fusion | bytes 8388616 | tf_op jit(solution)/shard_map/jit(dynamic_index_in_dim)/dynamic_slice | solution.py:38
  2.6 0.7 convolution_convert_fusion.3
  3.4 3.9 %collective-permute-start.3 = (bf16[8,256,128]{2,1,0:T(8,128)(2,1)S(1)}, bf16[8,256,128]{2,1,0:T(8,128)(2,1)S(1)}, u32[]{:S(2)}, u32[]{:S(2)}) collective-permute-start(bf16[8,256,128]{2,1,0:T(8,128)(2,1)S(1)} %convolution_convert_fusion.3), channel_id=1, source_target_pairs={{0,8},{1,9},{2,10},{3,11},{4,12},{5,13},{6,14},{7,15},{8,0},{9,1},... | collective-permute-start | bytes 1572872 | tf_op jit(solution)/shard_map/ppermute | solution.py:16
  7.3 0.7 convolution_convert_fusion.4
  8.4 32.4 %collective-permute-done.3 = bf16[8,256,128]{2,1,0:T(8,128)(2,1)S(1)} collective-permute-done((bf16[8,256,128]{2,1,0:T(8,128)(2,1)S(1)}, bf16[8,256,128]{2,1,0:T(8,128)(2,1)S(1)}, u32[]{:S(2)}, u32[]{:S(2)}) %collective-permute-start.3) | collective-permute-done | bytes 524320 | tf_op jit(solution)/shard_map/ppermute | solution.py:16
  40.8 0.3 fusion.6
  41.1 1.9 collective-permute-start.4
  43.0 0.9 fusion.61
  43.9 5.4 %collective-permute-start.11 = (bf16[8,128,128]{2,1,0:T(8,128)(2,1)S(1)}, bf16[8,128,128]{2,1,0:T(8,128)(2,1)S(1)}, u32[]{:S(2)}, u32[]{:S(2)}) collective-permute-start(bf16[8,128,128]{2,1,0:T(8,128)(2,1)S(1)} %get-tuple-element.14), channel_id=1, source_target_pairs={{0,32},{16,48},{32,0},{48,16},{64,96},{80,112},{96,64},{112,80},{1... | collective-permute-start | bytes 786440 | tf_op jit(solution)/shard_map/ppermute | solution.py:16
  49.6 26.2 %collective-permute-done.4 = bf16[8,256,128]{2,1,0:T(8,128)(2,1)S(1)} collective-permute-done((bf16[8,256,128]{2,1,0:T(8,128)(2,1)S(1)}, bf16[8,256,128]{2,1,0:T(8,128)(2,1)S(1)}, u32[]{:S(2)}, u32[]{:S(2)}) %collective-permute-start.4) | collective-permute-done | bytes 524320 | tf_op jit(solution)/shard_map/ppermute | solution.py:16
  76.1 3.0 %collective-permute-start.5 = (bf16[8,256,128]{2,1,0:T(8,128)(2,1)S(1)}, bf16[8,256,128]{2,1,0:T(8,128)(2,1)S(1)}, u32[]{:S(2)}, u32[]{:S(2)}) collective-permute-start(bf16[8,256,128]{2,1,0:T(8,128)(2,1)S(1)} %fusion.7), channel_id=1, source_target_pairs={{0,2},{1,3},{2,0},{3,1},{4,6},{5,7},{6,4},{7,5},{8,10},{9,11},{10,... | collective-permute-start | bytes 1572872 | tf_op jit(solution)/shard_map/ppermute | solution.py:16
  79.1 0.3 fusion.35
  79.7 10.9 %collective-permute-done.5 = bf16[8,256,128]{2,1,0:T(8,128)(2,1)S(1)} collective-permute-done((bf16[8,256,128]{2,1,0:T(8,128)(2,1)S(1)}, bf16[8,256,128]{2,1,0:T(8,128)(2,1)S(1)}, u32[]{:S(2)}, u32[]{:S(2)}) %collective-permute-start.5) | collective-permute-done | bytes 524320 | tf_op jit(solution)/shard_map/ppermute | solution.py:16
  90.9 6.4 %collective-permute-start.6 = (bf16[8,256,128]{2,1,0:T(8,128)(2,1)S(1)}, bf16[8,256,128]{2,1,0:T(8,128)(2,1)S(1)}, u32[]{:S(2)}, u32[]{:S(2)}) collective-permute-start(bf16[8,256,128]{2,1,0:T(8,128)(2,1)S(1)} %fusion.8), channel_id=1, source_target_pairs={{0,32},{16,48},{32,0},{48,16},{64,96},{80,112},{96,64},{112,80},{1... | collective-permute-start | bytes 1572872 | tf_op jit(solution)/shard_map/ppermute | solution.py:16
  98.0 17.9 %collective-permute-done.6 = bf16[8,256,128]{2,1,0:T(8,128)(2,1)S(1)} collective-permute-done((bf16[8,256,128]{2,1,0:T(8,128)(2,1)S(1)}, bf16[8,256,128]{2,1,0:T(8,128)(2,1)S(1)}, u32[]{:S(2)}, u32[]{:S(2)}) %collective-permute-start.6) | collective-permute-done | bytes 524320 | tf_op jit(solution)/shard_map/ppermute | solution.py:16
  115.9 0.4 convolution_convert_fusion.2
  116.4 1.6 copy.84
  117.9 10.2 %all-to-all-start.2 = ((bf16[8,16,16,256]{3,2,1,0:T(8,128)(2,1)}), bf16[8,16,16,256]{3,2,1,0:T(8,128)(2,1)}, u32[]{:S(2)}, u32[]{:S(2)}) async-start(bf16[8,16,16,256]{3,2,1,0:T(8,128)(2,1)} %bitcast.111), calls=%async_computation.2 | async-start | bytes 2097152 | tf_op jit(solution)/shard_map/all_to_all | solution.py:76
  128.1 1.7 collective-permute-done.1
  129.8 1.3 fusion.4
  131.1 3.2 %collective-permute-start.2 = (bf16[8,256,128]{2,1,0:T(8,128)(2,1)S(1)}, bf16[8,256,128]{2,1,0:T(8,128)(2,1)S(1)}, u32[]{:S(2)}, u32[]{:S(2)}) collective-permute-start(bf16[8,256,128]{2,1,0:T(8,128)(2,1)S(1)} %fusion.4), channel_id=1, source_target_pairs={{0,2},{1,3},{2,0},{3,1},{4,6},{5,7},{6,4},{7,5},{8,10},{9,11},{10,... | collective-permute-start | bytes 1572872 | tf_op jit(solution)/shard_map/ppermute | solution.py:16
  134.3 1.3 fusion.23
  135.6 8.5 %collective-permute-done.2 = bf16[8,256,128]{2,1,0:T(8,128)(2,1)S(1)} collective-permute-done((bf16[8,256,128]{2,1,0:T(8,128)(2,1)S(1)}, bf16[8,256,128]{2,1,0:T(8,128)(2,1)S(1)}, u32[]{:S(2)}, u32[]{:S(2)}) %collective-permute-start.2) | collective-permute-done | bytes 524320 | tf_op jit(solution)/shard_map/ppermute | solution.py:16
  144.1 2.7 %convolution_convert_fusion = bf16[8,256,640]{2,1,0:T(8,128)(2,1)S(1)} fusion(bf16[8,640,128]{2,1,0:T(8,128)(2,1)} %param.8, f32[8,256,128]{2,1,0:T(8,128)} %fusion.23, bf16[8,256,128]{2,1,0:T(8,128)(2,1)S(1)} %collective-permute-done.2, bf16[3,2,8,128,128]{4,3,2,1,0:T(8,128)(2,1)} %param.7), kind=kOutput, calls=%fused_computation.9 | convolution fusion | flops 404488192 | bytes 5767168 | tf_op jit(solution)/shard_map/mcr,mlr->mcl/dot_general | solution.py:71
  146.8 3.0 %copy.82 = bf16[16,8,16,640]{3,0,2,1:T(8,128)(2,1)} copy(bf16[16,8,16,640]{3,2,1,0:T(8,128)(2,1)S(1)} %bitcast.106) | data formatting | bytes 5242880 | tf_op jit(solution)/shard_map/reshape | solution.py:74
  149.8 7.6 %all-to-all-start = ((bf16[8,16,16,640]{3,2,1,0:T(8,128)(2,1)}), bf16[8,16,16,640]{3,2,1,0:T(8,128)(2,1)}, u32[]{:S(2)}, u32[]{:S(2)}) async-start(bf16[8,16,16,640]{3,2,1,0:T(8,128)(2,1)} %bitcast.103), calls=%async_computation | async-start | bytes 5242880 | tf_op jit(solution)/shard_map/all_to_all | solution.py:76
  157.4 3.7 %collective-permute-start.9 = (bf16[8,128,128]{2,1,0:T(8,128)(2,1)S(1)}, bf16[8,128,128]{2,1,0:T(8,128)(2,1)S(1)}, u32[]{:S(2)}, u32[]{:S(2)}) collective-permute-start(bf16[8,128,128]{2,1,0:T(8,128)(2,1)S(1)} %copy-done.8), channel_id=1, source_target_pairs={{0,32},{16,48},{32,0},{48,16},{64,96},{80,112},{96,64},{112,80},{1... | collective-permute-start | bytes 786440 | tf_op jit(solution)/shard_map/ppermute | solution.py:16
  161.1 1.7 collective-permute-start.8
  162.8 3.7 %collective-permute-start.7 = (bf16[8,128,128]{2,1,0:T(8,128)(2,1)S(1)}, bf16[8,128,128]{2,1,0:T(8,128)(2,1)}, u32[]{:S(2)}, u32[]{:S(2)}) collective-permute-start(bf16[8,128,128]{2,1,0:T(8,128)(2,1)S(1)} %get-tuple-element.11), channel_id=1, source_target_pairs={{0,32},{16,48},{32,0},{48,16},{64,96},{80,112},{96,64},{112,80},{1... | collective-permute-start | bytes 786440 | tf_op jit(solution)/shard_map/ppermute | solution.py:16
  166.5 0.6 multiply_convert_fusion.1
  167.4 7.2 %collective-permute-done.9 = bf16[8,128,128]{2,1,0:T(8,128)(2,1)S(1)} collective-permute-done((bf16[8,128,128]{2,1,0:T(8,128)(2,1)S(1)}, bf16[8,128,128]{2,1,0:T(8,128)(2,1)S(1)}, u32[]{:S(2)}, u32[]{:S(2)}) %collective-permute-start.9) | collective-permute-done | bytes 262176 | tf_op jit(solution)/shard_map/ppermute | solution.py:16
  174.5 11.5 %collective-permute-done.8 = bf16[8,128,128]{2,1,0:T(8,128)(2,1)S(1)} collective-permute-done((bf16[8,128,128]{2,1,0:T(8,128)(2,1)S(1)}, bf16[8,128,128]{2,1,0:T(8,128)(2,1)S(1)}, u32[]{:S(2)}, u32[]{:S(2)}) %collective-permute-start.8) | collective-permute-done | bytes 262176 | tf_op jit(solution)/shard_map/ppermute | solution.py:16
  186.0 0.7 copy-done.9
  186.7 10.8 %collective-permute-done.7 = bf16[8,128,128]{2,1,0:T(8,128)(2,1)} collective-permute-done((bf16[8,128,128]{2,1,0:T(8,128)(2,1)S(1)}, bf16[8,128,128]{2,1,0:T(8,128)(2,1)}, u32[]{:S(2)}, u32[]{:S(2)}) %collective-permute-start.7) | collective-permute-done | bytes 262176 | tf_op jit(solution)/shard_map/ppermute | solution.py:16
  197.5 1.6 convolution_convert_fusion.1
  199.1 2.1 copy.83
  201.2 5.5 %all-to-all-start.1 = ((bf16[8,16,16,384]{3,2,1,0:T(8,128)(2,1)}), bf16[8,16,16,384]{3,2,1,0:T(8,128)(2,1)}, u32[]{:S(2)}, u32[]{:S(2)}) async-start(bf16[8,16,16,384]{3,2,1,0:T(8,128)(2,1)} %bitcast.104), calls=%async_computation.1 | async-start | bytes 3145728 | tf_op jit(solution)/shard_map/all_to_all | solution.py:76
  206.7 3.3 %convolution_bitcast_fusion = f32[256,16,640]{2,0,1:T(8,128)S(1)} fusion(bf16[8,16,256,1]{2,1,3,0:T(8,128)(2,1)S(1)} %bitcast.117, bf16[8,16,16,640]{3,2,1,0:T(8,128)(2,1)} %all-to-all-done), kind=kOutput, calls=%fused_computation.2 | convolution fusion | flops 671088640 | bytes 13172736 | tf_op jit(solution)/shard_map/sak,sfal->kfl/dot_general | solution.py:84
  210.0 2.7 %slice_add_fusion.1 = f32[256,16,256]{2,0,1:T(8,128)S(1)} fusion(f32[256,16,640]{2,0,1:T(8,128)S(1)} %convolution_bitcast_fusion, bf16[8,16,256,1]{2,1,3,0:T(8,128)(2,1)S(1)} %bitcast.115, bf16[8,16,16,256]{3,2,1,0:T(8,128)(2,1)} %all-to-all-done.2), kind=kOutput, calls=%fused_computation.1 | convolution fusion | flops 269484032 | bytes 9502720 | tf_op jit(solution)/shard_map/sak,sfal->kfl/dot_general | solution.py:84
  212.7 1.3 copy-done.11
  214.0 1.7 fusion.60
  215.8 11.6 %all-to-all-done.1 = bf16[8,16,16,384]{3,2,1,0:T(8,128)(2,1)} async-done(((bf16[8,16,16,384]{3,2,1,0:T(8,128)(2,1)}), bf16[8,16,16,384]{3,2,1,0:T(8,128)(2,1)}, u32[]{:S(2)}, u32[]{:S(2)}) %all-to-all-start.1) | async-done | bytes 1572896 | tf_op jit(solution)/shard_map/all_to_all | solution.py:76
  227.4 4.3 %slice_add_fusion = f32[256,16,384]{2,0,1:T(8,128)S(1)} fusion(f32[256,16,640]{2,0,1:T(8,128)} %copy-done.11, bf16[8,16,256,1]{2,1,3,0:T(8,128)(2,1)S(1)} %bitcast.116, bf16[8,16,16,384]{3,2,1,0:T(8,128)(2,1)} %all-to-all-done.1), kind=kOutput, calls=%fused_computation | convolution fusion | flops 404226048 | bytes 14221312 | tf_op jit(solution)/shard_map/sak,sfal->kfl/dot_general | solution.py:84
  231.7 0.6 fusion.59
  232.3 1.0 copy-done.2
  233.3 2.5 %fusion.9 = bf16[256,8,256]{2,1,0:T(8,128)(2,1)S(1)} fusion(f32[256,8,1,256]{3,0,2,1:T(8,128)S(1)} %copy-done.2, f32[256,8,1,256]{3,0,2,1:T(8,128)S(1)} %get-tuple-element.7), kind=kLoop, calls=%fused_computation.28 | loop fusion | flops 1048576 | bytes 5242880 | tf_op jit(solution)/shard_map/convert_element_type | solution.py:92
  235.8 3.6 %fusion.2 = bf16[256,8,384]{2,1,0:T(8,128)(2,1)S(1)} fusion(f32[256,8,1,384]{3,0,2,1:T(8,128)S(1)} %get-tuple-element.6, f32[256,8,1,384]{3,0,2,1:T(8,128)S(1)} %get-tuple-element.5), kind=kLoop, calls=%fused_computation.11 | loop fusion | flops 1572864 | bytes 7864320 | tf_op jit(solution)/shard_map/convert_element_type | solution.py:92
  239.4 1.8 pad_maximum_fusion
  (41 shorter events, 2.6 us)
Async XLA Ops:
  0.0 2.6 %copy-start = (bf16[8,128,512]{2,1,0:T(8,128)(2,1)S(1)}, bf16[8,128,512]{2,1,0:T(8,128)(2,1)}, u32[]{:S(2)}) copy-start(bf16[8,128,512]{2,1,0:T(8,128)(2,1)} %param.6) | copy-start | bytes 3145732
  3.4 4.7 %copy-start.3 = (bf16[3,2,8,128,128]{4,3,2,1,0:T(8,128)(2,1)S(1)}, bf16[3,2,8,128,128]{4,3,2,1,0:T(8,128)(2,1)}, u32[]{:S(2)}) copy-start(bf16[3,2,8,128,128]{4,3,2,1,0:T(8,128)(2,1)} %param.7) | copy-start | bytes 4718596
  3.4 37.4 %collective-permute-start.3 = (bf16[8,256,128]{2,1,0:T(8,128)(2,1)S(1)}, bf16[8,256,128]{2,1,0:T(8,128)(2,1)S(1)}, u32[]{:S(2)}, u32[]{:S(2)}) collective-permute-start(bf16[8,256,128]{2,1,0:T(8,128)(2,1)S(1)} %convolution_convert_fusion.3), channel_id=1, source_target_pairs={{0,8},{1,9},{2,10},{3,11},{4,12},{5,13},{6,14},{7,15},{8,0},{9,1},... | collective-permute-start | bytes 1572872 | tf_op jit(solution)/shard_map/ppermute | solution.py:16
  8.0 35.0 %copy-start.4 = (bf16[8,640,128]{2,1,0:T(8,128)(2,1)S(1)}, bf16[8,640,128]{2,1,0:T(8,128)(2,1)}, u32[]{:S(2)}) copy-start(bf16[8,640,128]{2,1,0:T(8,128)(2,1)} %param.8) | copy-start | bytes 3932164
  8.0 89.3 %collective-permute-start = (bf16[8,256,128]{2,1,0:T(8,128)(2,1)S(1)}, bf16[8,256,128]{2,1,0:T(8,128)(2,1)S(1)}, u32[]{:S(2)}, u32[]{:S(2)}) collective-permute-start(bf16[8,256,128]{2,1,0:T(8,128)(2,1)S(1)} %convolution_convert_fusion.4), channel_id=1, source_target_pairs={{0,8},{1,9},{2,10},{3,11},{4,12},{5,13},{6,14},{7,15},{8,0},{9,1},... | collective-permute-start | bytes 1572872 | tf_op jit(solution)/shard_map/ppermute | solution.py:16
  41.1 34.8 %collective-permute-start.4 = (bf16[8,256,128]{2,1,0:T(8,128)(2,1)S(1)}, bf16[8,256,128]{2,1,0:T(8,128)(2,1)S(1)}, u32[]{:S(2)}, u32[]{:S(2)}) collective-permute-start(bf16[8,256,128]{2,1,0:T(8,128)(2,1)S(1)} %fusion.6), channel_id=1, source_target_pairs={{0,4},{1,5},{2,6},{3,7},{4,0},{5,1},{6,2},{7,3},{8,12},{9,13},{10,... | collective-permute-start | bytes 1572872 | tf_op jit(solution)/shard_map/ppermute | solution.py:16
  43.9 54.1 %collective-permute-start.11 = (bf16[8,128,128]{2,1,0:T(8,128)(2,1)S(1)}, bf16[8,128,128]{2,1,0:T(8,128)(2,1)S(1)}, u32[]{:S(2)}, u32[]{:S(2)}) collective-permute-start(bf16[8,128,128]{2,1,0:T(8,128)(2,1)S(1)} %get-tuple-element.14), channel_id=1, source_target_pairs={{0,32},{16,48},{32,0},{48,16},{64,96},{80,112},{96,64},{112,80},{1... | collective-permute-start | bytes 786440 | tf_op jit(solution)/shard_map/ppermute | solution.py:16
  49.3 48.7 %collective-permute-start.10 = (bf16[8,128,128]{2,1,0:T(8,128)(2,1)S(1)}, bf16[8,128,128]{2,1,0:T(8,128)(2,1)S(1)}, u32[]{:S(2)}, u32[]{:S(2)}) collective-permute-start(bf16[8,128,128]{2,1,0:T(8,128)(2,1)S(1)} %get-tuple-element.15), channel_id=1, source_target_pairs={{0,32},{16,48},{32,0},{48,16},{64,96},{80,112},{96,64},{112,80},{1... | collective-permute-start | bytes 786440 | tf_op jit(solution)/shard_map/ppermute | solution.py:16
  76.1 14.5 %collective-permute-start.5 = (bf16[8,256,128]{2,1,0:T(8,128)(2,1)S(1)}, bf16[8,256,128]{2,1,0:T(8,128)(2,1)S(1)}, u32[]{:S(2)}, u32[]{:S(2)}) collective-permute-start(bf16[8,256,128]{2,1,0:T(8,128)(2,1)S(1)} %fusion.7), channel_id=1, source_target_pairs={{0,2},{1,3},{2,0},{3,1},{4,6},{5,7},{6,4},{7,5},{8,10},{9,11},{10,... | collective-permute-start | bytes 1572872 | tf_op jit(solution)/shard_map/ppermute | solution.py:16
  90.9 25.0 %collective-permute-start.6 = (bf16[8,256,128]{2,1,0:T(8,128)(2,1)S(1)}, bf16[8,256,128]{2,1,0:T(8,128)(2,1)S(1)}, u32[]{:S(2)}, u32[]{:S(2)}) collective-permute-start(bf16[8,256,128]{2,1,0:T(8,128)(2,1)S(1)} %fusion.8), channel_id=1, source_target_pairs={{0,32},{16,48},{32,0},{48,16},{64,96},{80,112},{96,64},{112,80},{1... | collective-permute-start | bytes 1572872 | tf_op jit(solution)/shard_map/ppermute | solution.py:16
  97.6 32.2 %collective-permute-start.1 = (bf16[8,256,128]{2,1,0:T(8,128)(2,1)S(1)}, bf16[8,256,128]{2,1,0:T(8,128)(2,1)}, u32[]{:S(2)}, u32[]{:S(2)}) collective-permute-start(bf16[8,256,128]{2,1,0:T(8,128)(2,1)S(1)} %fusion.3), channel_id=1, source_target_pairs={{0,4},{1,5},{2,6},{3,7},{4,0},{5,1},{6,2},{7,3},{8,12},{9,13},{10,... | collective-permute-start | bytes 1572872 | tf_op jit(solution)/shard_map/ppermute | solution.py:16
  115.9 2.0 copy-start.5
  117.9 31.8 %all-to-all-start.2 = ((bf16[8,16,16,256]{3,2,1,0:T(8,128)(2,1)}), bf16[8,16,16,256]{3,2,1,0:T(8,128)(2,1)}, u32[]{:S(2)}, u32[]{:S(2)}) async-start(bf16[8,16,16,256]{3,2,1,0:T(8,128)(2,1)} %bitcast.111), calls=%async_computation.2 | async-start | bytes 2097152 | tf_op jit(solution)/shard_map/all_to_all | solution.py:76
  131.1 13.0 %collective-permute-start.2 = (bf16[8,256,128]{2,1,0:T(8,128)(2,1)S(1)}, bf16[8,256,128]{2,1,0:T(8,128)(2,1)S(1)}, u32[]{:S(2)}, u32[]{:S(2)}) collective-permute-start(bf16[8,256,128]{2,1,0:T(8,128)(2,1)S(1)} %fusion.4), channel_id=1, source_target_pairs={{0,2},{1,3},{2,0},{3,1},{4,6},{5,7},{6,4},{7,5},{8,10},{9,11},{10,... | collective-permute-start | bytes 1572872 | tf_op jit(solution)/shard_map/ppermute | solution.py:16
  149.8 7.6 %copy-start.8 = (bf16[8,128,128]{2,1,0:T(8,128)(2,1)S(1)}, bf16[8,128,128]{2,1,0:T(8,128)(2,1)}, u32[]{:S(2)}) copy-start(bf16[8,128,128]{2,1,0:T(8,128)(2,1)} %get-tuple-element.12) | copy-start | bytes 786436
  149.8 11.4 %copy-start.7 = (bf16[8,128,128]{2,1,0:T(8,128)(2,1)S(1)}, bf16[8,128,128]{2,1,0:T(8,128)(2,1)}, u32[]{:S(2)}) copy-start(bf16[8,128,128]{2,1,0:T(8,128)(2,1)} %get-tuple-element.13) | copy-start | bytes 786436
  149.8 16.7 %copy-start.10 = (s32[128]{0:T(128)S(1)}, s32[128]{0:T(128)}, u32[]{:S(2)}) copy-start(s32[128]{0:T(128)} %param.9) | copy-start | bytes 1540
  149.8 47.7 %copy-start.6 = (bf16[8,256,128]{2,1,0:T(8,128)(2,1)S(1)}, bf16[8,256,128]{2,1,0:T(8,128)(2,1)}, u32[]{:S(2)}) copy-start(bf16[8,256,128]{2,1,0:T(8,128)(2,1)} %copy-done.5) | copy-start | bytes 1572868
  149.8 51.4 %all-to-all-start = ((bf16[8,16,16,640]{3,2,1,0:T(8,128)(2,1)}), bf16[8,16,16,640]{3,2,1,0:T(8,128)(2,1)}, u32[]{:S(2)}, u32[]{:S(2)}) async-start(bf16[8,16,16,640]{3,2,1,0:T(8,128)(2,1)} %bitcast.103), calls=%async_computation | async-start | bytes 5242880 | tf_op jit(solution)/shard_map/all_to_all | solution.py:76
  157.4 17.1 %collective-permute-start.9 = (bf16[8,128,128]{2,1,0:T(8,128)(2,1)S(1)}, bf16[8,128,128]{2,1,0:T(8,128)(2,1)S(1)}, u32[]{:S(2)}, u32[]{:S(2)}) collective-permute-start(bf16[8,128,128]{2,1,0:T(8,128)(2,1)S(1)} %copy-done.8), channel_id=1, source_target_pairs={{0,32},{16,48},{32,0},{48,16},{64,96},{80,112},{96,64},{112,80},{1... | collective-permute-start | bytes 786440 | tf_op jit(solution)/shard_map/ppermute | solution.py:16
  161.1 24.9 %collective-permute-start.8 = (bf16[8,128,128]{2,1,0:T(8,128)(2,1)S(1)}, bf16[8,128,128]{2,1,0:T(8,128)(2,1)S(1)}, u32[]{:S(2)}, u32[]{:S(2)}) collective-permute-start(bf16[8,128,128]{2,1,0:T(8,128)(2,1)S(1)} %copy-done.7), channel_id=1, source_target_pairs={{0,32},{16,48},{32,0},{48,16},{64,96},{80,112},{96,64},{112,80},{1... | collective-permute-start | bytes 786440 | tf_op jit(solution)/shard_map/ppermute | solution.py:16
  162.8 34.7 %collective-permute-start.7 = (bf16[8,128,128]{2,1,0:T(8,128)(2,1)S(1)}, bf16[8,128,128]{2,1,0:T(8,128)(2,1)}, u32[]{:S(2)}, u32[]{:S(2)}) collective-permute-start(bf16[8,128,128]{2,1,0:T(8,128)(2,1)S(1)} %get-tuple-element.11), channel_id=1, source_target_pairs={{0,32},{16,48},{32,0},{48,16},{64,96},{80,112},{96,64},{112,80},{1... | collective-permute-start | bytes 786440 | tf_op jit(solution)/shard_map/ppermute | solution.py:16
  186.0 0.7 copy-start.9
  201.2 26.2 %all-to-all-start.1 = ((bf16[8,16,16,384]{3,2,1,0:T(8,128)(2,1)}), bf16[8,16,16,384]{3,2,1,0:T(8,128)(2,1)}, u32[]{:S(2)}, u32[]{:S(2)}) async-start(bf16[8,16,16,384]{3,2,1,0:T(8,128)(2,1)} %bitcast.104), calls=%async_computation.1 | async-start | bytes 3145728 | tf_op jit(solution)/shard_map/all_to_all | solution.py:76
  210.0 4.0 %copy-start.11 = (f32[256,16,640]{2,0,1:T(8,128)}, f32[256,16,640]{2,0,1:T(8,128)S(1)}, u32[]{:S(2)}) copy-start(f32[256,16,640]{2,0,1:T(8,128)S(1)} %convolution_bitcast_fusion) | copy-start | bytes 31457284
  231.7 1.6 copy-start.2
  235.7 5.4 %copy-start.1 = (bf16[8,128,512]{2,1,0:T(8,128)(2,1)S(1)}, bf16[8,128,512]{2,1,0:T(8,128)(2,1)}, u32[]{:S(2)}) copy-start(bf16[8,128,512]{2,1,0:T(8,128)(2,1)} %param.6) | copy-start | bytes 3145732

commit v2 on v1

v2 whole, which is shorter than its diff:
```python
import math

import jax
import jax.numpy as jnp
from jax import lax
from jax.experimental import pallas as pl
from jax.experimental.pallas import tpu as pltpu
from jax.sharding import PartitionSpec as P


PERIOD = 16384
NLON = 256
SPLIT = 384
PIECE = 128


def xor_permute(shard, axis, mask):
    return lax.ppermute(shard, axis, [(i, i ^ mask) for i in range(lax.axis_size(axis))])


def synthesis_table(order_ids, count, period):
    steps = jnp.arange(count, dtype=jnp.int32)
    phase = (order_ids[:, None] * steps[None, :] % period).astype(jnp.float32) * (
        2.0 * math.pi / period
    )
    weight = jnp.where(order_ids == 0, 1.0, 2.0).astype(jnp.float32)[:, None]
    table = jnp.stack([weight * jnp.cos(phase), -weight * jnp.sin(phase)], axis=1)
    return table.astype(jnp.bfloat16)


def latitude_values(reduced, factors, parts):
    m, count, rank = reduced.shape
    cols = count // parts
    lats = sum(f.shape[1] for f in factors)
    steps = lats // PIECE
    per = steps // len(factors)

    def body(reduced_ref, *refs):
        factor_refs, out_ref, wide = refs[: len(factors)], refs[-2], refs[-1]
        for j, factor_ref in enumerate(factor_refs):
            for i in range(per):
                for o in range(m):
                    acc = lax.dot_general(
                        reduced_ref[o],
                        factor_ref[o, i * PIECE : (i + 1) * PIECE],
                        (((1,), (1,)), ((), ())),
                        preferred_element_type=jnp.float32,
                    )
                    for p in range(parts):
                        wide[pl.ds(o * parts + p, cols, stride=m * parts), :] = acc[
                            p * cols : (p + 1) * cols
                        ]
                start = (j * per + i) * PIECE
                out_ref[:, :, start : start + PIECE] = (
                    wide[...].reshape(cols, m * parts, PIECE).astype(jnp.bfloat16)
                )

    flops = 2 * m * count * rank * lats
    return pl.pallas_call(
        body,
        out_shape=jax.ShapeDtypeStruct((cols, m * parts, lats), jnp.bfloat16),
        in_specs=[pl.BlockSpec(memory_space=pltpu.VMEM)] * (1 + len(factors)),
        out_specs=pl.BlockSpec(memory_space=pltpu.VMEM),
        scratch_shapes=[pltpu.VMEM((cols * m * parts, PIECE), jnp.float32)],
        compiler_params=pltpu.CompilerParams(vmem_limit_bytes=32 << 20),
        cost_estimate=pl.CostEstimate(flops=flops, bytes_accessed=2 * cols * m * parts * lats, transcendentals=0),
        name="latitude_values",
    )(reduced, *factors)


def field_products(table, near_values, far_values, first, out):
    half, group, mp, lats = near_values.shape
    nlon, depth = table.shape
    steps = far_values.shape[-1] // PIECE
    pairs = group // 2

    def body(table_ref, near_ref, far_ref, *refs):
        out_ref, wide = refs[-2], refs[-1]
        for p in range(pairs):
            sides = [
                jnp.concatenate(
                    [ref[:, f].reshape(half * mp, PIECE) for ref in (near_ref, far_ref)], 0
                )
                for f in (2 * p, 2 * p + 1)
            ]
            grid = jnp.dot(
                table_ref[...], jnp.concatenate(sides, 1), preferred_element_type=jnp.float32
            )
            wide[pl.ds(p, nlon, stride=pairs), :] = grid[:, :PIECE] * grid[:, PIECE:]
        out_ref[...] = wide[...].reshape(nlon, pairs, PIECE).astype(jnp.bfloat16)

    block = (half, group, mp, PIECE)
    in_specs = [
        pl.BlockSpec((nlon, depth), lambda i: (0, 0)),
        pl.BlockSpec(block, lambda i: (0, 0, 0, first + i)),
        pl.BlockSpec(block, lambda i: (0, 0, 0, i)),
    ]
    args, aliases = [table, near_values, far_values], {}
    if out is not None:
        in_specs.append(pl.BlockSpec(memory_space=pl.ANY))
        args.append(out)
        aliases = {3: 0}
    return pl.pallas_call(
        body,
        grid=(steps,),
        out_shape=jax.ShapeDtypeStruct((nlon, pairs, lats), jnp.bfloat16),
        in_specs=in_specs,
        out_specs=pl.BlockSpec((nlon, pairs, PIECE), lambda i: (0, 0, first + i)),
        scratch_shapes=[pltpu.VMEM((nlon * pairs, PIECE), jnp.float32)],
        input_output_aliases=aliases,
        compiler_params=pltpu.CompilerParams(vmem_limit_bytes=32 << 20),
        cost_estimate=pl.CostEstimate(
            flops=2 * nlon * depth * group * PIECE * steps,
            bytes_accessed=6 * nlon * pairs * PIECE * steps,
            transcendentals=0,
        ),
        name="field_products",
    )(*args)


def per_device(coefficients, leaf_factors, level_interpolants, latitude_factors, order_ids):
    m, parts, fields, leaf = coefficients.shape
    size = lax.axis_size("ord")
    group = fields // size
    half = size // 2
    side = (lax.axis_index("ord") >> 1) & 1
    by_side = coefficients.reshape(m, parts, size // 4, 2, 2 * group, leaf)

    def leaves(which):
        chosen = lax.dynamic_index_in_dim(by_side, which, 3, keepdims=False)
        flat = chosen.reshape(m, parts * half * group, leaf)
        return jnp.einsum(
            "mcl,mrl->mcr", flat, leaf_factors, preferred_element_type=jnp.float32
        ).astype(jnp.bfloat16)

    top = lax.axis_size("blk") // 2

    def level(k, here, there):
        mixed = jnp.einsum(
            "mcx,mhx->mch", here, level_interpolants[k, 0], preferred_element_type=jnp.float32
        ) + jnp.einsum(
            "mcx,mhx->mch", there, level_interpolants[k, 1], preferred_element_type=jnp.float32
        )
        return mixed.astype(jnp.bfloat16)

    near, far = leaves(side), leaves(1 - side)
    crossing = lambda shard: xor_permute(shard, "ord", 2)
    pieces = [crossing(latitude_factors[:, :SPLIT]), crossing(latitude_factors[:, SPLIT:])]
    for k in range(level_interpolants.shape[0]):
        near = level(k, near, xor_permute(near, "blk", top >> k))
        far = level(k, far, xor_permute(far, "blk", top >> k))
    crossed = crossing(far)
    groups = [[i for i in range(size) if (i >> 1) & 1 == s] for s in (0, 1)]

    def regroup(reduced, factors):
        values = latitude_values(reduced, factors, parts)
        values = values.reshape((half, group) + values.shape[1:])
        return lax.all_to_all(values, "ord", 0, 0, axis_index_groups=groups, tiled=True)

    table = synthesis_table(order_ids, NLON, PERIOD).reshape(size // 4, 2, 2 * m * parts, NLON)

    def rows(which):
        return lax.dynamic_index_in_dim(table, which, 1, keepdims=False).reshape(half * m * parts, NLON)

    both = jnp.concatenate([rows(side), rows(1 - side)], 0).T
    near_values = regroup(near, [latitude_factors])
    first = regroup(crossed, pieces[:1])
    second = regroup(crossed, pieces[1:])
    out = field_products(both, near_values, first, 0, None)
    return field_products(both, near_values, second, SPLIT // PIECE, out)


def solution(mesh):
    in_specs = (
        P("ord", None, None, "blk"),
        P("ord", None, "blk"),
        P(None, None, "ord", None, "blk"),
        P("ord", "blk", None),
        P(),
    )
    out_specs = P(None, "ord", "blk")

    return jax.shard_map(per_device, mesh=mesh, in_specs=in_specs, out_specs=out_specs, check_vma=False)
```

time: 242 us -> 221 us (0.913)
  matrix products: 21.7 us -> 8.05 us
  Pallas kernels: 0 us -> 11.7 us
  local copies, waits for them, and re-layouts: 15.8 us -> 7.84 us
  other arithmetic: 8.51 us -> 0.64 us
  starting transfers between devices: 56.4 us -> 50 us
  waiting for transfers between devices: 139 us -> 143 us
    dot_general x6 -> x0, matrix products: 15 us -> none  [the longest x3 10.3 us: partial_grid(): jnp.einsum('sak,sfal->kfl', rows(which), values, preferred_element_type=j...]
    pallas_call x0 -> x5, Pallas kernels: none -> 11.7 us  [the longest x2 7.07 us: field_products(): pl.pallas_call(body, grid=(steps,), out_shape=jax.ShapeDtypeStruct((nlon,...]
    all_to_all x3, starting transfers between devices: 23.3 us -> 16.4 us  [regroup(): lax.all_to_all(values, 'ord', 0, 0, axis_index_groups=groups, tiled=True)]
    reshape x3 -> x2, local copies, waits for them, and re-layouts: 6.66 us -> 0.23 us  [rows(): lax.dynamic_index_in_dim(table, which, 1, keepdims=False)]
    convert_element_type x2 -> x0, other arithmetic: 6.12 us -> none  [per_device(): outs.append((grid[:, :, 0, :] * grid[:, :, 1, :]).astype(jnp.bfloat16))]
    all_to_all x3, waiting for transfers between devices: 11.6 us -> 14.1 us  [regroup(): lax.all_to_all(values, 'ord', 0, 0, axis_index_groups=groups, tiled=True)]
    ppermute x12 -> x9, waiting for transfers between devices: 127 us -> 128 us  [xor_permute(): lax.ppermute(shard, axis, [(i, i ^ mask) for i in range(lax.axis_size(axi...]
    ppermute x12 -> x9, starting transfers between devices: 33.1 us -> 33.6 us  [xor_permute(): lax.ppermute(shard, axis, [(i, i ^ mask) for i in range(lax.axis_size(axi...]
  transfers between devices with their start and end apart: 15 -> 12, of which waited for: 10 -> 9; matrix products, arithmetic and copies ran while one was open for 11% -> 4% of each run, Pallas kernels for 0% -> 4%
where the time goes in v2:
time: 221 us
  waiting for transfers between devices  143 us (65%)
  starting transfers between devices  50 us (23%)
  Pallas kernels  11.7 us (5%)
  matrix products  8.05 us (4%)
  local copies, waits for them, and re-layouts  7.84 us (4%)
    ppermute x9, waiting for transfers between devices, xor_permute(): lax.ppermute(shard, axis, [(i, i ^ mask) for i in range(lax.axis_size(axi...  128 us
    ppermute x9, starting transfers between devices, xor_permute(): lax.ppermute(shard, axis, [(i, i ^ mask) for i in range(lax.axis_size(axi...  33.6 us
    all_to_all x3, starting transfers between devices, regroup(): lax.all_to_all(values, 'ord', 0, 0, axis_index_groups=groups, tiled=True)  16.4 us
    all_to_all x3, waiting for transfers between devices, regroup(): lax.all_to_all(values, 'ord', 0, 0, axis_index_groups=groups, tiled=True)  14.1 us
    pallas_call x2, Pallas kernels, field_products(): pl.pallas_call(body, grid=(steps,), out_shape=jax.ShapeDtypeStruct((nlon,...  7.07 us
    pallas_call x3, Pallas kernels, latitude_values(): pl.pallas_call(body, out_shape=jax.ShapeDtypeStruct((cols, m * parts, lat...  4.66 us
  transfers between devices with their start and end apart: 12, of which 9 were waited for; matrix products, arithmetic and copies ran while one was open for 4% of the time, Pallas kernels for 4%

profile of v2, /device:TPU:1, one launch (start us, length us, event | category | flops | bytes accessed | tf_op | source)
XLA Modules:
  0.0 221.0 jit_solution(8324363072219492307)
XLA Ops:
  0.0 2.6 %constant_dynamic-slice_fusion = (bf16[8,2,4,1,32,512]{5,4,3,2,1,0:T(8,128)(2,1)S(1)}, bf16[8,2,4,1,32,512]{5,4,3,2,1,0:T(8,128)(2,1)S(1)}) fusion(bf16[8,2,4,2,32,512]{5,4,3,2,1,0:T(8,128)(2,1)} %bitcast.63, s32[]{:T(128)S(6)} %select_n.35, s32[]{:T(128)S(6)} %select_n.34), kind=kLoop, calls=%fused_computation.58 | loop fusion | bytes 8388616 | tf_op jit(solution)/shard_map/jit(dynamic_index_in_dim)/dynamic_slice | solution.py:130
  2.7 0.7 convolution_convert_fusion
  3.4 3.9 %collective-permute-start.3 = (bf16[8,256,128]{2,1,0:T(8,128)(2,1)S(1)}, bf16[8,256,128]{2,1,0:T(8,128)(2,1)S(1)}, u32[]{:S(2)}, u32[]{:S(2)}) collective-permute-start(bf16[8,256,128]{2,1,0:T(8,128)(2,1)S(1)} %convolution_convert_fusion), channel_id=1, source_target_pairs={{0,8},{1,9},{2,10},{3,11},{4,12},{5,13},{6,14},{7,15},{8,0},{9,1},... | collective-permute-start | bytes 1572872 | tf_op jit(solution)/shard_map/ppermute | solution.py:18
  7.3 0.3 fusion.20
  7.6 22.0 %collective-permute-done.3 = bf16[8,256,128]{2,1,0:T(8,128)(2,1)S(1)} collective-permute-done((bf16[8,256,128]{2,1,0:T(8,128)(2,1)S(1)}, bf16[8,256,128]{2,1,0:T(8,128)(2,1)S(1)}, u32[]{:S(2)}, u32[]{:S(2)}) %collective-permute-start.3) | collective-permute-done | bytes 524320 | tf_op jit(solution)/shard_map/ppermute | solution.py:18
  29.5 0.3 fusion.3
  29.9 1.9 collective-permute-start.4
  31.8 5.5 %collective-permute-start.8 = (bf16[8,384,128]{2,1,0:T(8,128)(2,1)S(1)}, bf16[8,384,128]{2,1,0:T(8,128)(2,1)S(1)}, u32[]{:S(2)}, u32[]{:S(2)}) collective-permute-start(bf16[8,384,128]{2,1,0:T(8,128)(2,1)S(1)} %slice.37), channel_id=1, source_target_pairs={{0,32},{16,48},{32,0},{48,16},{64,96},{80,112},{96,64},{112,80},{1... | collective-permute-start | bytes 2359304 | tf_op jit(solution)/shard_map/ppermute | solution.py:18
  37.3 0.3 fusion.14
  37.6 4.9 %collective-permute-done.4 = bf16[8,256,128]{2,1,0:T(8,128)(2,1)S(1)} collective-permute-done((bf16[8,256,128]{2,1,0:T(8,128)(2,1)S(1)}, bf16[8,256,128]{2,1,0:T(8,128)(2,1)S(1)}, u32[]{:S(2)}, u32[]{:S(2)}) %collective-permute-start.4) | collective-permute-done | bytes 524320 | tf_op jit(solution)/shard_map/ppermute | solution.py:18
  42.5 0.3 fusion.4
  42.8 3.2 %collective-permute-start.5 = (bf16[8,256,128]{2,1,0:T(8,128)(2,1)S(1)}, bf16[8,256,128]{2,1,0:T(8,128)(2,1)S(1)}, u32[]{:S(2)}, u32[]{:S(2)}) collective-permute-start(bf16[8,256,128]{2,1,0:T(8,128)(2,1)S(1)} %fusion.4), channel_id=1, source_target_pairs={{0,2},{1,3},{2,0},{3,1},{4,6},{5,7},{6,4},{7,5},{8,10},{9,11},{10,... | collective-permute-start | bytes 1572872 | tf_op jit(solution)/shard_map/ppermute | solution.py:18
  46.1 0.7 convolution_convert_fusion.1
  46.8 4.0 %collective-permute-start = (bf16[8,256,128]{2,1,0:T(8,128)(2,1)S(1)}, bf16[8,256,128]{2,1,0:T(8,128)(2,1)S(1)}, u32[]{:S(2)}, u32[]{:S(2)}) collective-permute-start(bf16[8,256,128]{2,1,0:T(8,128)(2,1)S(1)} %convolution_convert_fusion.1), channel_id=1, source_target_pairs={{0,8},{1,9},{2,10},{3,11},{4,12},{5,13},{6,14},{7,15},{8,0},{9,1},... | collective-permute-start | bytes 1572872 | tf_op jit(solution)/shard_map/ppermute | solution.py:18
  50.7 0.3 fusion.8
  51.0 3.2 %collective-permute-done.5 = bf16[8,256,128]{2,1,0:T(8,128)(2,1)S(1)} collective-permute-done((bf16[8,256,128]{2,1,0:T(8,128)(2,1)S(1)}, bf16[8,256,128]{2,1,0:T(8,128)(2,1)S(1)}, u32[]{:S(2)}, u32[]{:S(2)}) %collective-permute-start.5) | collective-permute-done | bytes 524320 | tf_op jit(solution)/shard_map/ppermute | solution.py:18
  54.2 0.3 fusion.5
  54.5 7.7 %collective-permute-start.6 = (bf16[8,256,128]{2,1,0:T(8,128)(2,1)S(1)}, bf16[8,256,128]{2,1,0:T(8,128)(2,1)S(1)}, u32[]{:S(2)}, u32[]{:S(2)}) collective-permute-start(bf16[8,256,128]{2,1,0:T(8,128)(2,1)S(1)} %fusion.5), channel_id=1, source_target_pairs={{0,32},{16,48},{32,0},{48,16},{64,96},{80,112},{96,64},{112,80},{1... | collective-permute-start | bytes 1572872 | tf_op jit(solution)/shard_map/ppermute | solution.py:18
  62.2 0.3 fusion.22
  62.5 63.1 %collective-permute-done = bf16[8,256,128]{2,1,0:T(8,128)(2,1)S(1)} collective-permute-done((bf16[8,256,128]{2,1,0:T(8,128)(2,1)S(1)}, bf16[8,256,128]{2,1,0:T(8,128)(2,1)S(1)}, u32[]{:S(2)}, u32[]{:S(2)}) %collective-permute-start) | collective-permute-done | bytes 524320 | tf_op jit(solution)/shard_map/ppermute | solution.py:18
  125.6 1.1 fusion
  126.7 1.4 latitude_values.5
  128.2 1.2 copy-done.2
  129.4 4.8 %all-to-all-start.2 = ((bf16[8,16,16,384]{3,2,1,0:T(8,128)(2,1)}), bf16[8,16,16,384]{3,2,1,0:T(8,128)(2,1)S(1)}, u32[]{:S(2)}, u32[]{:S(2)}) async-start(bf16[8,16,16,384]{3,2,1,0:T(8,128)(2,1)} %bitcast.61), calls=%async_computation.2 | async-start | bytes 3145728 | tf_op jit(solution)/shard_map/all_to_all | solution.py:158
  134.1 1.5 fusion.16
  135.7 4.4 %collective-permute-done.1 = bf16[8,256,128]{2,1,0:T(8,128)(2,1)} collective-permute-done((bf16[8,256,128]{2,1,0:T(8,128)(2,1)}, bf16[8,256,128]{2,1,0:T(8,128)(2,1)}, u32[]{:S(2)}, u32[]{:S(2)}) %collective-permute-start.1) | collective-permute-done | bytes 524320 | tf_op jit(solution)/shard_map/ppermute | solution.py:18
  140.0 1.3 fusion.1
  141.4 3.2 %collective-permute-start.2 = (bf16[8,256,128]{2,1,0:T(8,128)(2,1)S(1)}, bf16[8,256,128]{2,1,0:T(8,128)(2,1)S(1)}, u32[]{:S(2)}, u32[]{:S(2)}) collective-permute-start(bf16[8,256,128]{2,1,0:T(8,128)(2,1)S(1)} %fusion.1), channel_id=1, source_target_pairs={{0,2},{1,3},{2,0},{3,1},{4,6},{5,7},{6,4},{7,5},{8,10},{9,11},{10,... | collective-permute-start | bytes 1572872 | tf_op jit(solution)/shard_map/ppermute | solution.py:18
  144.6 0.3 fusion.10
  144.9 10.4 %collective-permute-done.2 = bf16[8,256,128]{2,1,0:T(8,128)(2,1)S(1)} collective-permute-done((bf16[8,256,128]{2,1,0:T(8,128)(2,1)S(1)}, bf16[8,256,128]{2,1,0:T(8,128)(2,1)S(1)}, u32[]{:S(2)}, u32[]{:S(2)}) %collective-permute-start.2) | collective-permute-done | bytes 524320 | tf_op jit(solution)/shard_map/ppermute | solution.py:18
  155.3 0.3 fusion.2.reduced_ref
  155.6 2.3 %latitude_values.3 = bf16[128,16,640]{2,1,0:T(8,128)(2,1)S(1)} custom-call(bf16[8,256,128]{2,1,0:T(8,128)(2,1)S(1)} %fusion.2.reduced_ref, bf16[8,640,128]{2,1,0:T(8,128)(2,1)S(1)} %copy-done.4), custom_call_target="tpu_custom_call" | custom-call | flops 335544320 | bytes 2621440 | tf_op jit(solution)/shard_map/latitude_values/pallas_call | solution.py:59
  157.9 1.5 copy-done.1
  159.4 6.5 %all-to-all-start = ((bf16[8,16,16,640]{3,2,1,0:T(8,128)(2,1)}), bf16[8,16,16,640]{3,2,1,0:T(8,128)(2,1)}, u32[]{:S(2)}, u32[]{:S(2)}) async-start(bf16[8,16,16,640]{3,2,1,0:T(8,128)(2,1)} %bitcast.60), calls=%async_computation | async-start | bytes 5242880 | tf_op jit(solution)/shard_map/all_to_all | solution.py:158
  165.9 1.1 slice.36
  166.9 4.3 %collective-permute-start.7 = (bf16[8,256,128]{2,1,0:T(8,128)(2,1)S(1)}, bf16[8,256,128]{2,1,0:T(8,128)(2,1)S(1)}, u32[]{:S(2)}, u32[]{:S(2)}) collective-permute-start(bf16[8,256,128]{2,1,0:T(8,128)(2,1)S(1)} %slice.36), channel_id=1, source_target_pairs={{0,32},{16,48},{32,0},{48,16},{64,96},{80,112},{96,64},{112,80},{1... | collective-permute-start | bytes 1572872 | tf_op jit(solution)/shard_map/ppermute | solution.py:18
  171.2 20.5 %collective-permute-done.7.refs_0_ = bf16[8,256,128]{2,1,0:T(8,128)(2,1)S(1)} collective-permute-done((bf16[8,256,128]{2,1,0:T(8,128)(2,1)S(1)}, bf16[8,256,128]{2,1,0:T(8,128)(2,1)S(1)}, u32[]{:S(2)}, u32[]{:S(2)}) %collective-permute-start.7) | collective-permute-done | bytes 524320 | tf_op jit(solution)/shard_map/ppermute | solution.py:18
  191.7 1.0 latitude_values.4
  192.7 1.0 copy-done.5
  193.6 4.2 %all-to-all-done.near_ref = bf16[8,16,16,640]{3,2,1,0:T(8,128)(2,1)} async-done(((bf16[8,16,16,640]{3,2,1,0:T(8,128)(2,1)}), bf16[8,16,16,640]{3,2,1,0:T(8,128)(2,1)}, u32[]{:S(2)}, u32[]{:S(2)}) %all-to-all-start) | async-done | bytes 2621472 | tf_op jit(solution)/shard_map/all_to_all | solution.py:158
  197.8 5.1 %all-to-all-start.1 = ((bf16[8,16,16,256]{3,2,1,0:T(8,128)(2,1)}), bf16[8,16,16,256]{3,2,1,0:T(8,128)(2,1)}, u32[]{:S(2)}, u32[]{:S(2)}) async-start(bf16[8,16,16,256]{3,2,1,0:T(8,128)(2,1)} %bitcast.62), calls=%async_computation.1 | async-start | bytes 2097152 | tf_op jit(solution)/shard_map/all_to_all | solution.py:158
  202.9 0.6 multiply_convert_fusion.1
  203.5 0.1 copy.13
  203.8 0.1 copy.14
  203.9 0.1 copy.15
  204.0 4.1 %field_products.2.refs_0_ = bf16[256,8,640]{2,1,0:T(8,128)(2,1)} custom-call(bf16[256,256]{1,0:T(8,128)(2,1)S(1)} %maximum_bitcast_fusion.table_ref, bf16[8,16,16,640]{3,2,1,0:T(8,128)(2,1)} %all-to-all-done.near_ref, bf16[8,16,16,384]{3,2,1,0:T(8,128)(2,1)S(1)} %all-to-all-done.2.far_ref), custom_call_target="tpu_custom_call" | custom-call | flops 805306368 | bytes 4718592 | tf_op jit(solution)/shard_map/field_products/pallas_call | solution.py:103
  208.1 9.9 %all-to-all-done.1.far_ref = bf16[8,16,16,256]{3,2,1,0:T(8,128)(2,1)} async-done(((bf16[8,16,16,256]{3,2,1,0:T(8,128)(2,1)}), bf16[8,16,16,256]{3,2,1,0:T(8,128)(2,1)}, u32[]{:S(2)}, u32[]{:S(2)}) %all-to-all-start.1) | async-done | bytes 1048608 | tf_op jit(solution)/shard_map/all_to_all | solution.py:158
  218.0 3.0 %field_products.3 = bf16[256,8,640]{2,1,0:T(8,128)(2,1)} custom-call(bf16[256,256]{1,0:T(8,128)(2,1)S(1)} %maximum_bitcast_fusion.table_ref, bf16[8,16,16,640]{3,2,1,0:T(8,128)(2,1)} %all-to-all-done.near_ref, bf16[8,16,16,256]{3,2,1,0:T(8,128)(2,1)} %all-to-all-done.1.far_ref, ...), custom_call_target="tpu_custom_call", output_to_operand_aliasing={{}: (3, {})} | custom-call | flops 536870912 | bytes 3145728 | tf_op jit(solution)/shard_map/field_products/pallas_call | solution.py:103
  (25 shorter events, 0.2 us)
Async XLA Ops:
  0.0 2.6 %copy-start = (bf16[8,128,512]{2,1,0:T(8,128)(2,1)S(1)}, bf16[8,128,512]{2,1,0:T(8,128)(2,1)}, u32[]{:S(2)}) copy-start(bf16[8,128,512]{2,1,0:T(8,128)(2,1)} %param.6) | copy-start | bytes 3145732
  2.6 4.6 %copy-start.6 = (bf16[3,2,8,128,128]{4,3,2,1,0:T(8,128)(2,1)S(1)}, bf16[3,2,8,128,128]{4,3,2,1,0:T(8,128)(2,1)}, u32[]{:S(2)}) copy-start(bf16[3,2,8,128,128]{4,3,2,1,0:T(8,128)(2,1)} %param.7) | copy-start | bytes 4718596
  3.4 26.2 %collective-permute-start.3 = (bf16[8,256,128]{2,1,0:T(8,128)(2,1)S(1)}, bf16[8,256,128]{2,1,0:T(8,128)(2,1)S(1)}, u32[]{:S(2)}, u32[]{:S(2)}) collective-permute-start(bf16[8,256,128]{2,1,0:T(8,128)(2,1)S(1)} %convolution_convert_fusion), channel_id=1, source_target_pairs={{0,8},{1,9},{2,10},{3,11},{4,12},{5,13},{6,14},{7,15},{8,0},{9,1},... | collective-permute-start | bytes 1572872 | tf_op jit(solution)/shard_map/ppermute | solution.py:18
  7.6 24.2 %copy-start.3 = (bf16[8,640,128]{2,1,0:T(8,128)(2,1)S(1)}, bf16[8,640,128]{2,1,0:T(8,128)(2,1)}, u32[]{:S(2)}) copy-start(bf16[8,640,128]{2,1,0:T(8,128)(2,1)} %refs_0_.1) | copy-start | bytes 3932164
  29.9 12.7 %collective-permute-start.4 = (bf16[8,256,128]{2,1,0:T(8,128)(2,1)S(1)}, bf16[8,256,128]{2,1,0:T(8,128)(2,1)S(1)}, u32[]{:S(2)}, u32[]{:S(2)}) collective-permute-start(bf16[8,256,128]{2,1,0:T(8,128)(2,1)S(1)} %fusion.3), channel_id=1, source_target_pairs={{0,4},{1,5},{2,6},{3,7},{4,0},{5,1},{6,2},{7,3},{8,12},{9,13},{10,... | collective-permute-start | bytes 1572872 | tf_op jit(solution)/shard_map/ppermute | solution.py:18
  31.8 94.9 %collective-permute-start.8 = (bf16[8,384,128]{2,1,0:T(8,128)(2,1)S(1)}, bf16[8,384,128]{2,1,0:T(8,128)(2,1)S(1)}, u32[]{:S(2)}, u32[]{:S(2)}) collective-permute-start(bf16[8,384,128]{2,1,0:T(8,128)(2,1)S(1)} %slice.37), channel_id=1, source_target_pairs={{0,32},{16,48},{32,0},{48,16},{64,96},{80,112},{96,64},{112,80},{1... | collective-permute-start | bytes 2359304 | tf_op jit(solution)/shard_map/ppermute | solution.py:18
  42.8 11.4 %collective-permute-start.5 = (bf16[8,256,128]{2,1,0:T(8,128)(2,1)S(1)}, bf16[8,256,128]{2,1,0:T(8,128)(2,1)S(1)}, u32[]{:S(2)}, u32[]{:S(2)}) collective-permute-start(bf16[8,256,128]{2,1,0:T(8,128)(2,1)S(1)} %fusion.4), channel_id=1, source_target_pairs={{0,2},{1,3},{2,0},{3,1},{4,6},{5,7},{6,4},{7,5},{8,10},{9,11},{10,... | collective-permute-start | bytes 1572872 | tf_op jit(solution)/shard_map/ppermute | solution.py:18
  46.8 78.8 %collective-permute-start = (bf16[8,256,128]{2,1,0:T(8,128)(2,1)S(1)}, bf16[8,256,128]{2,1,0:T(8,128)(2,1)S(1)}, u32[]{:S(2)}, u32[]{:S(2)}) collective-permute-start(bf16[8,256,128]{2,1,0:T(8,128)(2,1)S(1)} %convolution_convert_fusion.1), channel_id=1, source_target_pairs={{0,8},{1,9},{2,10},{3,11},{4,12},{5,13},{6,14},{7,15},{8,0},{9,1},... | collective-permute-start | bytes 1572872 | tf_op jit(solution)/shard_map/ppermute | solution.py:18
  54.5 72.2 %collective-permute-start.6 = (bf16[8,256,128]{2,1,0:T(8,128)(2,1)S(1)}, bf16[8,256,128]{2,1,0:T(8,128)(2,1)S(1)}, u32[]{:S(2)}, u32[]{:S(2)}) collective-permute-start(bf16[8,256,128]{2,1,0:T(8,128)(2,1)S(1)} %fusion.5), channel_id=1, source_target_pairs={{0,32},{16,48},{32,0},{48,16},{64,96},{80,112},{96,64},{112,80},{1... | collective-permute-start | bytes 1572872 | tf_op jit(solution)/shard_map/ppermute | solution.py:18
  126.7 13.3 %collective-permute-start.1 = (bf16[8,256,128]{2,1,0:T(8,128)(2,1)}, bf16[8,256,128]{2,1,0:T(8,128)(2,1)}, u32[]{:S(2)}, u32[]{:S(2)}) collective-permute-start(bf16[8,256,128]{2,1,0:T(8,128)(2,1)} %fusion), channel_id=1, source_target_pairs={{0,4},{1,5},{2,6},{3,7},{4,0},{5,1},{6,2},{7,3},{8,12},{9,13},{10,... | collective-permute-start | bytes 1572872 | tf_op jit(solution)/shard_map/ppermute | solution.py:18
  128.2 1.2 copy-start.2
  129.4 30.0 %all-to-all-start.2 = ((bf16[8,16,16,384]{3,2,1,0:T(8,128)(2,1)}), bf16[8,16,16,384]{3,2,1,0:T(8,128)(2,1)S(1)}, u32[]{:S(2)}, u32[]{:S(2)}) async-start(bf16[8,16,16,384]{3,2,1,0:T(8,128)(2,1)} %bitcast.61), calls=%async_computation.2 | async-start | bytes 3145728 | tf_op jit(solution)/shard_map/all_to_all | solution.py:158
  134.1 5.9 %copy-start.7 = (bf16[3,2,8,128,128]{4,3,2,1,0:T(8,128)(2,1)S(1)}, bf16[3,2,8,128,128]{4,3,2,1,0:T(8,128)(2,1)}, u32[]{:S(2)}) copy-start(bf16[3,2,8,128,128]{4,3,2,1,0:T(8,128)(2,1)} %param.7) | copy-start | bytes 4718596
  141.4 13.9 %collective-permute-start.2 = (bf16[8,256,128]{2,1,0:T(8,128)(2,1)S(1)}, bf16[8,256,128]{2,1,0:T(8,128)(2,1)S(1)}, u32[]{:S(2)}, u32[]{:S(2)}) collective-permute-start(bf16[8,256,128]{2,1,0:T(8,128)(2,1)S(1)} %fusion.1), channel_id=1, source_target_pairs={{0,2},{1,3},{2,0},{3,1},{4,6},{5,7},{6,4},{7,5},{8,10},{9,11},{10,... | collective-permute-start | bytes 1572872 | tf_op jit(solution)/shard_map/ppermute | solution.py:18
  144.9 10.7 %copy-start.4 = (bf16[8,640,128]{2,1,0:T(8,128)(2,1)S(1)}, bf16[8,640,128]{2,1,0:T(8,128)(2,1)}, u32[]{:S(2)}) copy-start(bf16[8,640,128]{2,1,0:T(8,128)(2,1)} %refs_0_.1) | copy-start | bytes 3932164
  157.9 1.5 copy-start.1
  159.4 38.4 %all-to-all-start = ((bf16[8,16,16,640]{3,2,1,0:T(8,128)(2,1)}), bf16[8,16,16,640]{3,2,1,0:T(8,128)(2,1)}, u32[]{:S(2)}, u32[]{:S(2)}) async-start(bf16[8,16,16,640]{3,2,1,0:T(8,128)(2,1)} %bitcast.60), calls=%async_computation | async-start | bytes 5242880 | tf_op jit(solution)/shard_map/all_to_all | solution.py:158
  166.9 24.7 %collective-permute-start.7 = (bf16[8,256,128]{2,1,0:T(8,128)(2,1)S(1)}, bf16[8,256,128]{2,1,0:T(8,128)(2,1)S(1)}, u32[]{:S(2)}, u32[]{:S(2)}) collective-permute-start(bf16[8,256,128]{2,1,0:T(8,128)(2,1)S(1)} %slice.36), channel_id=1, source_target_pairs={{0,32},{16,48},{32,0},{48,16},{64,96},{80,112},{96,64},{112,80},{1... | collective-permute-start | bytes 1572872 | tf_op jit(solution)/shard_map/ppermute | solution.py:18
  192.7 1.0 copy-start.5
  193.6 9.3 %copy-start.8 = (s32[128]{0:T(128)S(1)}, s32[128]{0:T(128)}, u32[]{:S(2)}) copy-start(s32[128]{0:T(128)} %param.9) | copy-start | bytes 1540
  197.8 20.2 %all-to-all-start.1 = ((bf16[8,16,16,256]{3,2,1,0:T(8,128)(2,1)}), bf16[8,16,16,256]{3,2,1,0:T(8,128)(2,1)}, u32[]{:S(2)}, u32[]{:S(2)}) async-start(bf16[8,16,16,256]{3,2,1,0:T(8,128)(2,1)} %bitcast.62), calls=%async_computation.1 | async-start | bytes 2097152 | tf_op jit(solution)/shard_map/all_to_all | solution.py:158

commit v3 on v2

--- a/solution.py
+++ b/solution.py
@@ -10,7 +10,7 @@
 
 PERIOD = 16384
 NLON = 256
-SPLIT = 384
+CUTS = (0, 384, 640)
 PIECE = 128
 
 
@@ -68,18 +68,60 @@
     )(reduced, *factors)
 
 
+def split_values(reduced, factors, parts, group, order):
+    m, count, rank = reduced.shape
+    cols = count // parts
+    dests = cols // group
+    lats = factors.shape[1]
+    mp = m * parts
+
+    def body(order_ref, reduced_ref, factor_ref, *refs):
+        outs, wide = refs[:-1], refs[-1]
+        for start in range(0, lats, PIECE):
+            for o in range(m):
+                acc = lax.dot_general(
+                    reduced_ref[o],
+                    factor_ref[o, start : start + PIECE],
+                    (((1,), (1,)), ((), ())),
+                    preferred_element_type=jnp.float32,
+                )
+                for p in range(parts):
+                    wide[pl.ds(o * parts + p, cols, stride=mp), :] = acc[p * cols : (p + 1) * cols]
+            for k, out_ref in enumerate(outs):
+                row = pl.multiple_of(order_ref[k] * (group * mp), group * mp)
+                chosen = wide[pl.ds(row, group * mp), :]
+                out_ref[:, :, start : start + PIECE] = chosen.reshape(group, mp, PIECE).astype(
+                    jnp.bfloat16
+                )
+
+    return list(pl.pallas_call(
+        body,
+        out_shape=[jax.ShapeDtypeStruct((group, mp, lats), jnp.bfloat16)] * dests,
+        in_specs=[pl.BlockSpec(memory_space=pltpu.SMEM)]
+        + [pl.BlockSpec(memory_space=pltpu.VMEM)] * 2,
+        out_specs=[pl.BlockSpec(memory_space=pltpu.VMEM)] * dests,
+        scratch_shapes=[pltpu.VMEM((cols * mp, PIECE), jnp.float32)],
+        compiler_params=pltpu.CompilerParams(vmem_limit_bytes=32 << 20),
+        cost_estimate=pl.CostEstimate(
+            flops=2 * m * count * rank * lats, bytes_accessed=2 * cols * mp * lats, transcendentals=0
+        ),
+        name="split_values",
+    )(order, reduced, factors))
+
+
 def field_products(table, near_values, far_values, first, out):
     half, group, mp, lats = near_values.shape
     nlon, depth = table.shape
-    steps = far_values.shape[-1] // PIECE
+    count = len(far_values)
+    steps = far_values[0].shape[-1] // PIECE
     pairs = group // 2
 
-    def body(table_ref, near_ref, far_ref, *refs):
-        out_ref, wide = refs[-2], refs[-1]
+    def body(table_ref, near_ref, *refs):
+        far_refs, out_ref, wide = refs[:count], refs[-2], refs[-1]
         for p in range(pairs):
             sides = [
                 jnp.concatenate(
-                    [ref[:, f].reshape(half * mp, PIECE) for ref in (near_ref, far_ref)], 0
+                    [ref[:, f].reshape(-1, PIECE) for ref in (near_ref, *far_refs)], 0
                 )
                 for f in (2 * p, 2 * p + 1)
             ]
@@ -93,13 +135,15 @@
     in_specs = [
         pl.BlockSpec((nlon, depth), lambda i: (0, 0)),
         pl.BlockSpec(block, lambda i: (0, 0, 0, first + i)),
-        pl.BlockSpec(block, lambda i: (0, 0, 0, i)),
     ]
-    args, aliases = [table, near_values, far_values], {}
+    in_specs += [
+        pl.BlockSpec((half // count, group, mp, PIECE), lambda i: (0, 0, 0, i)) for _ in range(count)
+    ]
+    args, aliases = [table, near_values, *far_values], {}
     if out is not None:
         in_specs.append(pl.BlockSpec(memory_space=pl.ANY))
         args.append(out)
-        aliases = {3: 0}
+        aliases = {2 + count: 0}
     return pl.pallas_call(
         body,
         grid=(steps,),
@@ -145,7 +189,7 @@
 
     near, far = leaves(side), leaves(1 - side)
     crossing = lambda shard: xor_permute(shard, "ord", 2)
-    pieces = [crossing(latitude_factors[:, :SPLIT]), crossing(latitude_factors[:, SPLIT:])]
+    pieces = [crossing(latitude_factors[:, begin:end]) for begin, end in zip(CUTS[:-1], CUTS[1:])]
     for k in range(level_interpolants.shape[0]):
         near = level(k, near, xor_permute(near, "blk", top >> k))
         far = level(k, far, xor_permute(far, "blk", top >> k))
@@ -162,12 +206,36 @@
     def rows(which):
         return lax.dynamic_index_in_dim(table, which, 1, keepdims=False).reshape(half * m * parts, NLON)
 
-    both = jnp.concatenate([rows(side), rows(1 - side)], 0).T
+    here, across = rows(side), rows(1 - side)
     near_values = regroup(near, [latitude_factors])
     first = regroup(crossed, pieces[:1])
-    second = regroup(crossed, pieces[1:])
-    out = field_products(both, near_values, first, 0, None)
-    return field_products(both, near_values, second, SPLIT // PIECE, out)
+    place = lax.axis_index("ord")
+    column, core = place >> 2, place & 1
+    quarter = size // 4
+    shifts = [(2, 0), (2, 1), (1, 0), (3, 0), (1, 1), (3, 1), (0, 1), (0, 0)]
+    to = jnp.stack([((column + a) % quarter) * 2 + (core ^ b) for a, b in shifts])
+    source = jnp.stack([((column - a) % quarter) * 2 + (core ^ b) for a, b in shifts])
+    to = to.astype(jnp.int32)
+    later = []
+    for factors in pieces[1:]:
+        chunks = split_values(crossed, factors, parts, group, to)
+        for k, (a, b) in enumerate(shifts):
+            if (a, b) != (0, 0):
+                pairs = [
+                    (i, (((i >> 2) + a) % quarter) * 4 + (i & 2) + ((i & 1) ^ b))
+                    for i in range(size)
+                ]
+                chunks[k] = lax.ppermute(chunks[k], "ord", pairs)
+        later.append([chunk[None] for chunk in chunks])
+    moved = jnp.take(
+        across.reshape(half, m * parts, NLON), source, axis=0, mode="clip"
+    ).reshape(across.shape)
+    out = field_products(jnp.concatenate([here, across], 0).T, near_values, [first], 0, None)
+    for i, chunks in enumerate(later):
+        out = field_products(
+            jnp.concatenate([here, moved], 0).T, near_values, chunks, CUTS[i + 1] // PIECE, out
+        )
+    return out
 
 
 def solution(mesh):

time: 221 us -> 223 us (level)
  waiting for transfers between devices: 143 us -> 128 us
  starting transfers between devices: 50 us -> 58 us
  local copies, waits for them, and re-layouts: 7.84 us -> 12.9 us
    all_to_all x3 -> x2, waiting for transfers between devices: 14.1 us -> 0.01 us  [regroup(): lax.all_to_all(values, 'ord', 0, 0, axis_index_groups=groups, tiled=True)]
    ppermute x0 -> x7, starting transfers between devices: none -> 13 us  [per_device(): chunks[k] = lax.ppermute(chunks[k], 'ord', pairs)]
    all_to_all x3 -> x2, starting transfers between devices: 16.4 us -> 11.4 us  [regroup(): lax.all_to_all(values, 'ord', 0, 0, axis_index_groups=groups, tiled=True)]
    pallas_call x0 -> x1, Pallas kernels: none -> 2.88 us  [split_values(): pl.pallas_call(body, out_shape=[jax.ShapeDtypeStruct((group, mp, lats), j...]
    unnamed x18 -> x24, local copies, waits for them, and re-layouts: 3.64 us -> 5.27 us
    pallas_call x3 -> x2, Pallas kernels: 4.66 us -> 3.68 us  [latitude_values(): pl.pallas_call(body, out_shape=jax.ShapeDtypeStruct((cols, m * parts, lat...]
  transfers between devices with their start and end apart: 12 -> 18, of which waited for: 9 -> 7; matrix products, arithmetic and copies ran while one was open for 4% -> 6% of each run, Pallas kernels for 4% -> 5%
where the time goes in v3:
time: 223 us; the launch traced here: 222 us
  waiting for transfers between devices  128 us (57%)
  starting transfers between devices  58 us (26%)
  Pallas kernels  13.5 us (6%)
  local copies, waits for them, and re-layouts  12.9 us (6%)
  matrix products  8.05 us (4%)
    ppermute x9, waiting for transfers between devices, xor_permute(): lax.ppermute(shard, axis, [(i, i ^ mask) for i in range(lax.axis_size(axi...  128 us
    ppermute x9, starting transfers between devices, xor_permute(): lax.ppermute(shard, axis, [(i, i ^ mask) for i in range(lax.axis_size(axi...  33.5 us
    ppermute x7, starting transfers between devices, per_device(): chunks[k] = lax.ppermute(chunks[k], 'ord', pairs)  13 us
    all_to_all x2, starting transfers between devices, regroup(): lax.all_to_all(values, 'ord', 0, 0, axis_index_groups=groups, tiled=True)  11.4 us
    pallas_call x2, Pallas kernels, field_products(): pl.pallas_call(body, grid=(steps,), out_shape=jax.ShapeDtypeStruct((nlon,...  6.94 us
    unnamed x24, local copies, waits for them, and re-layouts  5.27 us
  transfers between devices with their start and end apart: 18, of which 7 were waited for; matrix products, arithmetic and copies ran while one was open for 6% of the time, Pallas kernels for 5%

profile of v3, /device:TPU:1, one launch (start us, length us, event | category | flops | bytes accessed | tf_op | source)
XLA Modules:
  0.0 222.2 jit_solution(4159976592800060919)
XLA Ops:
  0.0 2.6 %constant_dynamic-slice_fusion = (bf16[8,2,4,1,32,512]{5,4,3,2,1,0:T(8,128)(2,1)S(1)}, bf16[8,2,4,1,32,512]{5,4,3,2,1,0:T(8,128)(2,1)S(1)}) fusion(bf16[8,2,4,2,32,512]{5,4,3,2,1,0:T(8,128)(2,1)} %bitcast.92, s32[]{:T(128)S(6)} %select_n.83, s32[]{:T(128)S(6)} %select_n.82), kind=kLoop, calls=%fused_computation.63 | loop fusion | bytes 8388616 | tf_op jit(solution)/shard_map/jit(dynamic_index_in_dim)/dynamic_slice | solution.py:174
  2.7 0.7 convolution_convert_fusion
  3.4 3.9 %collective-permute-start.3 = (bf16[8,256,128]{2,1,0:T(8,128)(2,1)S(1)}, bf16[8,256,128]{2,1,0:T(8,128)(2,1)S(1)}, u32[]{:S(2)}, u32[]{:S(2)}) collective-permute-start(bf16[8,256,128]{2,1,0:T(8,128)(2,1)S(1)} %convolution_convert_fusion), channel_id=1, source_target_pairs={{0,8},{1,9},{2,10},{3,11},{4,12},{5,13},{6,14},{7,15},{8,0},{9,1},... | collective-permute-start | bytes 1572872 | tf_op jit(solution)/shard_map/ppermute | solution.py:18
  7.6 22.0 %collective-permute-done.3 = bf16[8,256,128]{2,1,0:T(8,128)(2,1)S(1)} collective-permute-done((bf16[8,256,128]{2,1,0:T(8,128)(2,1)S(1)}, bf16[8,256,128]{2,1,0:T(8,128)(2,1)S(1)}, u32[]{:S(2)}, u32[]{:S(2)}) %collective-permute-start.3) | collective-permute-done | bytes 524320 | tf_op jit(solution)/shard_map/ppermute | solution.py:18
  29.5 0.3 fusion.3
  29.9 1.9 collective-permute-start.4
  31.8 5.5 %collective-permute-start.15 = (bf16[8,384,128]{2,1,0:T(8,128)(2,1)S(1)}, bf16[8,384,128]{2,1,0:T(8,128)(2,1)S(1)}, u32[]{:S(2)}, u32[]{:S(2)}) collective-permute-start(bf16[8,384,128]{2,1,0:T(8,128)(2,1)S(1)} %slice.37), channel_id=1, source_target_pairs={{0,32},{16,48},{32,0},{48,16},{64,96},{80,112},{96,64},{112,80},{1... | collective-permute-start | bytes 2359304 | tf_op jit(solution)/shard_map/ppermute | solution.py:18
  37.6 4.9 %collective-permute-done.4 = bf16[8,256,128]{2,1,0:T(8,128)(2,1)S(1)} collective-permute-done((bf16[8,256,128]{2,1,0:T(8,128)(2,1)S(1)}, bf16[8,256,128]{2,1,0:T(8,128)(2,1)S(1)}, u32[]{:S(2)}, u32[]{:S(2)}) %collective-permute-start.4) | collective-permute-done | bytes 524320 | tf_op jit(solution)/shard_map/ppermute | solution.py:18
  42.8 3.2 %collective-permute-start.5 = (bf16[8,256,128]{2,1,0:T(8,128)(2,1)S(1)}, bf16[8,256,128]{2,1,0:T(8,128)(2,1)S(1)}, u32[]{:S(2)}, u32[]{:S(2)}) collective-permute-start(bf16[8,256,128]{2,1,0:T(8,128)(2,1)S(1)} %fusion.4), channel_id=1, source_target_pairs={{0,2},{1,3},{2,0},{3,1},{4,6},{5,7},{6,4},{7,5},{8,10},{9,11},{10,... | collective-permute-start | bytes 1572872 | tf_op jit(solution)/shard_map/ppermute | solution.py:18
  46.1 0.7 convolution_convert_fusion.1
  46.8 4.0 %collective-permute-start = (bf16[8,256,128]{2,1,0:T(8,128)(2,1)S(1)}, bf16[8,256,128]{2,1,0:T(8,128)(2,1)S(1)}, u32[]{:S(2)}, u32[]{:S(2)}) collective-permute-start(bf16[8,256,128]{2,1,0:T(8,128)(2,1)S(1)} %convolution_convert_fusion.1), channel_id=1, source_target_pairs={{0,8},{1,9},{2,10},{3,11},{4,12},{5,13},{6,14},{7,15},{8,0},{9,1},... | collective-permute-start | bytes 1572872 | tf_op jit(solution)/shard_map/ppermute | solution.py:18
  51.1 3.2 %collective-permute-done.5 = bf16[8,256,128]{2,1,0:T(8,128)(2,1)S(1)} collective-permute-done((bf16[8,256,128]{2,1,0:T(8,128)(2,1)S(1)}, bf16[8,256,128]{2,1,0:T(8,128)(2,1)S(1)}, u32[]{:S(2)}, u32[]{:S(2)}) %collective-permute-start.5) | collective-permute-done | bytes 524320 | tf_op jit(solution)/shard_map/ppermute | solution.py:18
  54.5 7.7 %collective-permute-start.6 = (bf16[8,256,128]{2,1,0:T(8,128)(2,1)S(1)}, bf16[8,256,128]{2,1,0:T(8,128)(2,1)S(1)}, u32[]{:S(2)}, u32[]{:S(2)}) collective-permute-start(bf16[8,256,128]{2,1,0:T(8,128)(2,1)S(1)} %fusion.5), channel_id=1, source_target_pairs={{0,32},{16,48},{32,0},{48,16},{64,96},{80,112},{96,64},{112,80},{1... | collective-permute-start | bytes 1572872 | tf_op jit(solution)/shard_map/ppermute | solution.py:18
  62.5 63.1 %collective-permute-done = bf16[8,256,128]{2,1,0:T(8,128)(2,1)S(1)} collective-permute-done((bf16[8,256,128]{2,1,0:T(8,128)(2,1)S(1)}, bf16[8,256,128]{2,1,0:T(8,128)(2,1)S(1)}, u32[]{:S(2)}, u32[]{:S(2)}) %collective-permute-start) | collective-permute-done | bytes 524320 | tf_op jit(solution)/shard_map/ppermute | solution.py:18
  125.6 1.1 fusion
  126.7 1.4 latitude_values.3
  128.2 1.2 copy-done.2
  129.4 4.8 %all-to-all-start.1 = ((bf16[8,16,16,384]{3,2,1,0:T(8,128)(2,1)}), bf16[8,16,16,384]{3,2,1,0:T(8,128)(2,1)S(1)}, u32[]{:S(2)}, u32[]{:S(2)}) async-start(bf16[8,16,16,384]{3,2,1,0:T(8,128)(2,1)} %bitcast.86), calls=%async_computation.1 | async-start | bytes 3145728 | tf_op jit(solution)/shard_map/all_to_all | solution.py:202
  134.1 1.5 fusion.16
  135.7 4.4 %collective-permute-done.1 = bf16[8,256,128]{2,1,0:T(8,128)(2,1)} collective-permute-done((bf16[8,256,128]{2,1,0:T(8,128)(2,1)}, bf16[8,256,128]{2,1,0:T(8,128)(2,1)}, u32[]{:S(2)}, u32[]{:S(2)}) %collective-permute-start.1) | collective-permute-done | bytes 524320 | tf_op jit(solution)/shard_map/ppermute | solution.py:18
  140.0 1.3 fusion.1
  141.4 3.2 %collective-permute-start.2 = (bf16[8,256,128]{2,1,0:T(8,128)(2,1)S(1)}, bf16[8,256,128]{2,1,0:T(8,128)(2,1)S(1)}, u32[]{:S(2)}, u32[]{:S(2)}) collective-permute-start(bf16[8,256,128]{2,1,0:T(8,128)(2,1)S(1)} %fusion.1), channel_id=1, source_target_pairs={{0,2},{1,3},{2,0},{3,1},{4,6},{5,7},{6,4},{7,5},{8,10},{9,11},{10,... | collective-permute-start | bytes 1572872 | tf_op jit(solution)/shard_map/ppermute | solution.py:18
  144.9 10.4 %collective-permute-done.2 = bf16[8,256,128]{2,1,0:T(8,128)(2,1)S(1)} collective-permute-done((bf16[8,256,128]{2,1,0:T(8,128)(2,1)S(1)}, bf16[8,256,128]{2,1,0:T(8,128)(2,1)S(1)}, u32[]{:S(2)}, u32[]{:S(2)}) %collective-permute-start.2) | collective-permute-done | bytes 524320 | tf_op jit(solution)/shard_map/ppermute | solution.py:18
  155.6 2.3 %latitude_values.2 = bf16[128,16,640]{2,1,0:T(8,128)(2,1)S(1)} custom-call(bf16[8,256,128]{2,1,0:T(8,128)(2,1)S(1)} %fusion.2.reduced_ref, bf16[8,640,128]{2,1,0:T(8,128)(2,1)S(1)} %copy-done.4), custom_call_target="tpu_custom_call" | custom-call | flops 335544320 | bytes 2621440 | tf_op jit(solution)/shard_map/latitude_values/pallas_call | solution.py:59
  157.9 1.5 copy-done.1
  159.4 6.6 %all-to-all-start = ((bf16[8,16,16,640]{3,2,1,0:T(8,128)(2,1)}), bf16[8,16,16,640]{3,2,1,0:T(8,128)(2,1)}, u32[]{:S(2)}, u32[]{:S(2)}) async-start(bf16[8,16,16,640]{3,2,1,0:T(8,128)(2,1)} %bitcast.85), calls=%async_computation | async-start | bytes 5242880 | tf_op jit(solution)/shard_map/all_to_all | solution.py:202
  166.0 1.9 slice.36
  167.9 4.2 %collective-permute-start.7 = (bf16[8,256,128]{2,1,0:T(8,128)(2,1)}, bf16[8,256,128]{2,1,0:T(8,128)(2,1)}, u32[]{:S(2)}, u32[]{:S(2)}) collective-permute-start(bf16[8,256,128]{2,1,0:T(8,128)(2,1)} %slice.36), channel_id=1, source_target_pairs={{0,32},{16,48},{32,0},{48,16},{64,96},{80,112},{96,64},{112,80},{1... | collective-permute-start | bytes 1572872 | tf_op jit(solution)/shard_map/ppermute | solution.py:18
  172.1 0.6 multiply_convert_fusion.1
  173.0 19.8 %collective-permute-done.7.factor_ref = bf16[8,256,128]{2,1,0:T(8,128)(2,1)} collective-permute-done((bf16[8,256,128]{2,1,0:T(8,128)(2,1)}, bf16[8,256,128]{2,1,0:T(8,128)(2,1)}, u32[]{:S(2)}, u32[]{:S(2)}) %collective-permute-start.7) | collective-permute-done | bytes 524320 | tf_op jit(solution)/shard_map/ppermute | solution.py:18
  192.8 2.9 %split_values.1 = (bf16[16,16,256]{2,1,0:T(8,128)(2,1)}, bf16[16,16,256]{2,1,0:T(8,128)(2,1)}, bf16[16,16,256]{2,1,0:T(8,128)(2,1)}, bf16[16,16,256]{2,1,0:T(8,1...) custom-call(s32[8]{0:T(128)S(1)} %stack.72.order_ref, ...), custom_call_target="tpu_custom_call" | custom-call | flops 134217728 | bytes 1048576 | tf_op jit(solution)/shard_map/split_values/pallas_call | solution.py:97
  195.7 0.6 copy-done.5
  196.4 0.6 copy-done.6
  197.0 0.6 copy-done.7
  197.7 0.6 copy-done.8
  198.3 2.6 %collective-permute-start.8 = (bf16[16,16,256]{2,1,0:T(8,128)(2,1)}, bf16[16,16,256]{2,1,0:T(8,128)(2,1)S(1)}, u32[]{:S(2)}, u32[]{:S(2)}) collective-permute-start(bf16[16,16,256]{2,1,0:T(8,128)(2,1)} %get-tuple-element.13), channel_id=1, source_target_pairs={{0,128},{16,144},{32,160},{48,176},{64,192},{80,208},{96,224},{112... | collective-permute-start | bytes 393224 | tf_op jit(solution)/shard_map/ppermute | solution.py:228
  200.9 4.1 %collective-permute-start.9 = (bf16[16,16,256]{2,1,0:T(8,128)(2,1)}, bf16[16,16,256]{2,1,0:T(8,128)(2,1)S(1)}, u32[]{:S(2)}, u32[]{:S(2)}) collective-permute-start(bf16[16,16,256]{2,1,0:T(8,128)(2,1)} %get-tuple-element.14), channel_id=1, source_target_pairs={{0,144},{16,128},{32,176},{48,160},{64,208},{80,192},{96,240},{112... | collective-permute-start | bytes 393224 | tf_op jit(solution)/shard_map/ppermute | solution.py:228
  205.2 0.7 copy.16
  206.0 0.6 gather_fusion
  206.5 0.7 copy.17
  207.3 0.7 copy.21
  208.0 1.4 collective-permute-start.10
  209.3 1.3 collective-permute-start.11
  210.7 3.0 %collective-permute-start.13 = (bf16[16,16,256]{2,1,0:T(8,128)(2,1)}, bf16[16,16,256]{2,1,0:T(8,128)(2,1)}, u32[]{:S(2)}, u32[]{:S(2)}) collective-permute-start(bf16[16,16,256]{2,1,0:T(8,128)(2,1)} %copy-done.6), channel_id=1, source_target_pairs={{0,208},{16,192},{32,240},{48,224},{64,16},{80,0},{96,48},{112,32}... | collective-permute-start | bytes 393224 | tf_op jit(solution)/shard_map/ppermute | solution.py:228
  213.6 0.6 collective-permute-start.14
  214.2 0.9 fusion.37
  215.2 4.1 %field_products.2.refs_8_ = bf16[256,8,640]{2,1,0:T(8,128)(2,1)} custom-call(bf16[256,256]{1,0:T(8,128)(2,1)S(1)} %get-tuple-element.25.table_ref, bf16[8,16,16,640]{3,2,1,0:T(8,128)(2,1)} %all-to-all-done.near_ref, bf16[8,16,16,384]{3,2,1,0:T(8,128)(2,1)S(1)} %all-to-all-done.1.refs_0_), custom_call_target="tpu_custom_call" | custom-call | flops 805306368 | bytes 4718592 | tf_op jit(solution)/shard_map/field_products/pallas_call | solution.py:147
  219.3 2.9 %field_products.3 = bf16[256,8,640]{2,1,0:T(8,128)(2,1)} custom-call(bf16[256,256]{1,0:T(8,128)(2,1)S(1)} %get-tuple-element.26.table_ref, bf16[8,16,16,640]{3,2,1,0:T(8,128)(2,1)} %all-to-all-done.near_ref, bf16[1,16,16,256]{3,2,1,0:T(8,128)(2,1)S(1)} %bitcast.88, bf16[1,16,16,256]{3,2,1,0:T(8,128)(2,1)S(1)} %bitcast.89, ...), custom_call_target="tpu_custom_call", output_to_operand_aliasing={{}: (10, {})} | custom-call | flops 536870912 | bytes 3145728 | tf_op jit(solution)/shard_map/field_products/pallas_call | solution.py:147
  (48 shorter events, 2.9 us)
Async XLA Ops:
  0.0 2.6 %copy-start = (bf16[8,128,512]{2,1,0:T(8,128)(2,1)S(1)}, bf16[8,128,512]{2,1,0:T(8,128)(2,1)}, u32[]{:S(2)}) copy-start(bf16[8,128,512]{2,1,0:T(8,128)(2,1)} %param.6) | copy-start | bytes 3145732
  2.6 4.6 %copy-start.9 = (bf16[3,2,8,128,128]{4,3,2,1,0:T(8,128)(2,1)S(1)}, bf16[3,2,8,128,128]{4,3,2,1,0:T(8,128)(2,1)}, u32[]{:S(2)}) copy-start(bf16[3,2,8,128,128]{4,3,2,1,0:T(8,128)(2,1)} %param.7) | copy-start | bytes 4718596
  3.4 26.2 %collective-permute-start.3 = (bf16[8,256,128]{2,1,0:T(8,128)(2,1)S(1)}, bf16[8,256,128]{2,1,0:T(8,128)(2,1)S(1)}, u32[]{:S(2)}, u32[]{:S(2)}) collective-permute-start(bf16[8,256,128]{2,1,0:T(8,128)(2,1)S(1)} %convolution_convert_fusion), channel_id=1, source_target_pairs={{0,8},{1,9},{2,10},{3,11},{4,12},{5,13},{6,14},{7,15},{8,0},{9,1},... | collective-permute-start | bytes 1572872 | tf_op jit(solution)/shard_map/ppermute | solution.py:18
  7.6 24.2 %copy-start.3 = (bf16[8,640,128]{2,1,0:T(8,128)(2,1)S(1)}, bf16[8,640,128]{2,1,0:T(8,128)(2,1)}, u32[]{:S(2)}) copy-start(bf16[8,640,128]{2,1,0:T(8,128)(2,1)} %refs_0_.1) | copy-start | bytes 3932164
  29.9 12.7 %collective-permute-start.4 = (bf16[8,256,128]{2,1,0:T(8,128)(2,1)S(1)}, bf16[8,256,128]{2,1,0:T(8,128)(2,1)S(1)}, u32[]{:S(2)}, u32[]{:S(2)}) collective-permute-start(bf16[8,256,128]{2,1,0:T(8,128)(2,1)S(1)} %fusion.3), channel_id=1, source_target_pairs={{0,4},{1,5},{2,6},{3,7},{4,0},{5,1},{6,2},{7,3},{8,12},{9,13},{10,... | collective-permute-start | bytes 1572872 | tf_op jit(solution)/shard_map/ppermute | solution.py:18
  31.8 94.9 %collective-permute-start.15 = (bf16[8,384,128]{2,1,0:T(8,128)(2,1)S(1)}, bf16[8,384,128]{2,1,0:T(8,128)(2,1)S(1)}, u32[]{:S(2)}, u32[]{:S(2)}) collective-permute-start(bf16[8,384,128]{2,1,0:T(8,128)(2,1)S(1)} %slice.37), channel_id=1, source_target_pairs={{0,32},{16,48},{32,0},{48,16},{64,96},{80,112},{96,64},{112,80},{1... | collective-permute-start | bytes 2359304 | tf_op jit(solution)/shard_map/ppermute | solution.py:18
  42.8 11.4 %collective-permute-start.5 = (bf16[8,256,128]{2,1,0:T(8,128)(2,1)S(1)}, bf16[8,256,128]{2,1,0:T(8,128)(2,1)S(1)}, u32[]{:S(2)}, u32[]{:S(2)}) collective-permute-start(bf16[8,256,128]{2,1,0:T(8,128)(2,1)S(1)} %fusion.4), channel_id=1, source_target_pairs={{0,2},{1,3},{2,0},{3,1},{4,6},{5,7},{6,4},{7,5},{8,10},{9,11},{10,... | collective-permute-start | bytes 1572872 | tf_op jit(solution)/shard_map/ppermute | solution.py:18
  46.8 78.8 %collective-permute-start = (bf16[8,256,128]{2,1,0:T(8,128)(2,1)S(1)}, bf16[8,256,128]{2,1,0:T(8,128)(2,1)S(1)}, u32[]{:S(2)}, u32[]{:S(2)}) collective-permute-start(bf16[8,256,128]{2,1,0:T(8,128)(2,1)S(1)} %convolution_convert_fusion.1), channel_id=1, source_target_pairs={{0,8},{1,9},{2,10},{3,11},{4,12},{5,13},{6,14},{7,15},{8,0},{9,1},... | collective-permute-start | bytes 1572872 | tf_op jit(solution)/shard_map/ppermute | solution.py:18
  54.5 72.2 %collective-permute-start.6 = (bf16[8,256,128]{2,1,0:T(8,128)(2,1)S(1)}, bf16[8,256,128]{2,1,0:T(8,128)(2,1)S(1)}, u32[]{:S(2)}, u32[]{:S(2)}) collective-permute-start(bf16[8,256,128]{2,1,0:T(8,128)(2,1)S(1)} %fusion.5), channel_id=1, source_target_pairs={{0,32},{16,48},{32,0},{48,16},{64,96},{80,112},{96,64},{112,80},{1... | collective-permute-start | bytes 1572872 | tf_op jit(solution)/shard_map/ppermute | solution.py:18
  126.7 13.3 %collective-permute-start.1 = (bf16[8,256,128]{2,1,0:T(8,128)(2,1)}, bf16[8,256,128]{2,1,0:T(8,128)(2,1)}, u32[]{:S(2)}, u32[]{:S(2)}) collective-permute-start(bf16[8,256,128]{2,1,0:T(8,128)(2,1)} %fusion), channel_id=1, source_target_pairs={{0,4},{1,5},{2,6},{3,7},{4,0},{5,1},{6,2},{7,3},{8,12},{9,13},{10,... | collective-permute-start | bytes 1572872 | tf_op jit(solution)/shard_map/ppermute | solution.py:18
  128.2 1.2 copy-start.2
  129.4 30.0 %all-to-all-start.1 = ((bf16[8,16,16,384]{3,2,1,0:T(8,128)(2,1)}), bf16[8,16,16,384]{3,2,1,0:T(8,128)(2,1)S(1)}, u32[]{:S(2)}, u32[]{:S(2)}) async-start(bf16[8,16,16,384]{3,2,1,0:T(8,128)(2,1)} %bitcast.86), calls=%async_computation.1 | async-start | bytes 3145728 | tf_op jit(solution)/shard_map/all_to_all | solution.py:202
  134.1 5.9 %copy-start.10 = (bf16[3,2,8,128,128]{4,3,2,1,0:T(8,128)(2,1)S(1)}, bf16[3,2,8,128,128]{4,3,2,1,0:T(8,128)(2,1)}, u32[]{:S(2)}) copy-start(bf16[3,2,8,128,128]{4,3,2,1,0:T(8,128)(2,1)} %param.7) | copy-start | bytes 4718596
  141.4 13.9 %collective-permute-start.2 = (bf16[8,256,128]{2,1,0:T(8,128)(2,1)S(1)}, bf16[8,256,128]{2,1,0:T(8,128)(2,1)S(1)}, u32[]{:S(2)}, u32[]{:S(2)}) collective-permute-start(bf16[8,256,128]{2,1,0:T(8,128)(2,1)S(1)} %fusion.1), channel_id=1, source_target_pairs={{0,2},{1,3},{2,0},{3,1},{4,6},{5,7},{6,4},{7,5},{8,10},{9,11},{10,... | collective-permute-start | bytes 1572872 | tf_op jit(solution)/shard_map/ppermute | solution.py:18
  144.9 10.7 %copy-start.4 = (bf16[8,640,128]{2,1,0:T(8,128)(2,1)S(1)}, bf16[8,640,128]{2,1,0:T(8,128)(2,1)}, u32[]{:S(2)}) copy-start(bf16[8,640,128]{2,1,0:T(8,128)(2,1)} %refs_0_.1) | copy-start | bytes 3932164
  157.9 1.5 copy-start.1
  159.4 12.7 %copy-start.11 = (s32[128]{0:T(128)S(1)}, s32[128]{0:T(128)}, u32[]{:S(2)}) copy-start(s32[128]{0:T(128)} %param.9) | copy-start | bytes 1540
  159.4 55.8 %all-to-all-start = ((bf16[8,16,16,640]{3,2,1,0:T(8,128)(2,1)}), bf16[8,16,16,640]{3,2,1,0:T(8,128)(2,1)}, u32[]{:S(2)}, u32[]{:S(2)}) async-start(bf16[8,16,16,640]{3,2,1,0:T(8,128)(2,1)} %bitcast.85), calls=%async_computation | async-start | bytes 5242880 | tf_op jit(solution)/shard_map/all_to_all | solution.py:202
  167.9 25.0 %collective-permute-start.7 = (bf16[8,256,128]{2,1,0:T(8,128)(2,1)}, bf16[8,256,128]{2,1,0:T(8,128)(2,1)}, u32[]{:S(2)}, u32[]{:S(2)}) collective-permute-start(bf16[8,256,128]{2,1,0:T(8,128)(2,1)} %slice.36), channel_id=1, source_target_pairs={{0,32},{16,48},{32,0},{48,16},{64,96},{80,112},{96,64},{112,80},{1... | collective-permute-start | bytes 1572872 | tf_op jit(solution)/shard_map/ppermute | solution.py:18
  195.7 0.7 copy-start.5
  196.4 0.6 copy-start.6
  197.0 0.6 copy-start.7
  197.7 0.6 copy-start.8
  198.3 12.4 %collective-permute-start.8 = (bf16[16,16,256]{2,1,0:T(8,128)(2,1)}, bf16[16,16,256]{2,1,0:T(8,128)(2,1)S(1)}, u32[]{:S(2)}, u32[]{:S(2)}) collective-permute-start(bf16[16,16,256]{2,1,0:T(8,128)(2,1)} %get-tuple-element.13), channel_id=1, source_target_pairs={{0,128},{16,144},{32,160},{48,176},{64,192},{80,208},{96,224},{112... | collective-permute-start | bytes 393224 | tf_op jit(solution)/shard_map/ppermute | solution.py:228
  200.9 12.7 %collective-permute-start.9 = (bf16[16,16,256]{2,1,0:T(8,128)(2,1)}, bf16[16,16,256]{2,1,0:T(8,128)(2,1)S(1)}, u32[]{:S(2)}, u32[]{:S(2)}) collective-permute-start(bf16[16,16,256]{2,1,0:T(8,128)(2,1)} %get-tuple-element.14), channel_id=1, source_target_pairs={{0,144},{16,128},{32,176},{48,160},{64,208},{80,192},{96,240},{112... | collective-permute-start | bytes 393224 | tf_op jit(solution)/shard_map/ppermute | solution.py:228
  208.0 11.3 %collective-permute-start.10 = (bf16[16,16,256]{2,1,0:T(8,128)(2,1)}, bf16[16,16,256]{2,1,0:T(8,128)(2,1)S(1)}, u32[]{:S(2)}, u32[]{:S(2)}) collective-permute-start(bf16[16,16,256]{2,1,0:T(8,128)(2,1)} %get-tuple-element.15), channel_id=1, source_target_pairs={{0,64},{16,80},{32,96},{48,112},{64,128},{80,144},{96,160},{112,17... | collective-permute-start | bytes 393224 | tf_op jit(solution)/shard_map/ppermute | solution.py:228
  209.3 9.9 %collective-permute-start.11 = (bf16[16,16,256]{2,1,0:T(8,128)(2,1)}, bf16[16,16,256]{2,1,0:T(8,128)(2,1)S(1)}, u32[]{:S(2)}, u32[]{:S(2)}) collective-permute-start(bf16[16,16,256]{2,1,0:T(8,128)(2,1)} %copy-done.8), channel_id=1, source_target_pairs={{0,192},{16,208},{32,224},{48,240},{64,0},{80,16},{96,32},{112,48}... | collective-permute-start | bytes 393224 | tf_op jit(solution)/shard_map/ppermute | solution.py:228
  210.6 8.6 %collective-permute-start.12 = (bf16[16,16,256]{2,1,0:T(8,128)(2,1)}, bf16[16,16,256]{2,1,0:T(8,128)(2,1)}, u32[]{:S(2)}, u32[]{:S(2)}) collective-permute-start(bf16[16,16,256]{2,1,0:T(8,128)(2,1)} %copy-done.7), channel_id=1, source_target_pairs={{0,80},{16,64},{32,112},{48,96},{64,144},{80,128},{96,176},{112,16... | collective-permute-start | bytes 393224 | tf_op jit(solution)/shard_map/ppermute | solution.py:228
  210.7 8.6 %collective-permute-start.13 = (bf16[16,16,256]{2,1,0:T(8,128)(2,1)}, bf16[16,16,256]{2,1,0:T(8,128)(2,1)}, u32[]{:S(2)}, u32[]{:S(2)}) collective-permute-start(bf16[16,16,256]{2,1,0:T(8,128)(2,1)} %copy-done.6), channel_id=1, source_target_pairs={{0,208},{16,192},{32,240},{48,224},{64,16},{80,0},{96,48},{112,32}... | collective-permute-start | bytes 393224 | tf_op jit(solution)/shard_map/ppermute | solution.py:228
  213.6 5.7 %collective-permute-start.14 = (bf16[16,16,256]{2,1,0:T(8,128)(2,1)}, bf16[16,16,256]{2,1,0:T(8,128)(2,1)}, u32[]{:S(2)}, u32[]{:S(2)}) collective-permute-start(bf16[16,16,256]{2,1,0:T(8,128)(2,1)} %copy-done.5), channel_id=1, source_target_pairs={{0,16},{16,0},{32,48},{48,32},{64,80},{80,64},{96,112},{112,96},{1... | collective-permute-start | bytes 393224 | tf_op jit(solution)/shard_map/ppermute | solution.py:228

commit v4 on v3

--- a/solution.py
+++ b/solution.py
@@ -170,8 +170,8 @@
     side = (lax.axis_index("ord") >> 1) & 1
     by_side = coefficients.reshape(m, parts, size // 4, 2, 2 * group, leaf)
 
-    def leaves(which):
-        chosen = lax.dynamic_index_in_dim(by_side, which, 3, keepdims=False)
+    def leaves(which, source):
+        chosen = lax.dynamic_index_in_dim(source, which, 3, keepdims=False)
         flat = chosen.reshape(m, parts * half * group, leaf)
         return jnp.einsum(
             "mcl,mrl->mcr", flat, leaf_factors, preferred_element_type=jnp.float32
@@ -187,7 +187,8 @@
         )
         return mixed.astype(jnp.bfloat16)
 
-    near, far = leaves(side), leaves(1 - side)
+    far = leaves(1 - side, by_side)
+    near = leaves(side, lax.optimization_barrier((by_side, far))[0])
     crossing = lambda shard: xor_permute(shard, "ord", 2)
     pieces = [crossing(latitude_factors[:, begin:end]) for begin, end in zip(CUTS[:-1], CUTS[1:])]
     for k in range(level_interpolants.shape[0]):

time: 223 us -> 229 us (1.027)
  local copies, waits for them, and re-layouts: 12.9 us -> 17.1 us
    unnamed x24 -> x28, local copies, waits for them, and re-layouts: 5.27 us -> 7.42 us
  transfers between devices with their start and end apart: 18 -> 18, of which waited for: 7 -> 7; matrix products, arithmetic and copies ran while one was open for 6% -> 8% of each run, Pallas kernels for 5% -> 5%
where the time goes in v4:
time: 229 us; the launch traced here: 228 us
  waiting for transfers between devices  126 us (55%)
  starting transfers between devices  59.7 us (26%)
  local copies, waits for them, and re-layouts  17.1 us (7%)
  Pallas kernels  13.5 us (6%)
  matrix products  10.1 us (4%)
    ppermute x9, waiting for transfers between devices, xor_permute(): lax.ppermute(shard, axis, [(i, i ^ mask) for i in range(lax.axis_size(axi...  126 us
    ppermute x9, starting transfers between devices, xor_permute(): lax.ppermute(shard, axis, [(i, i ^ mask) for i in range(lax.axis_size(axi...  33.2 us
    ppermute x7, starting transfers between devices, per_device(): chunks[k] = lax.ppermute(chunks[k], 'ord', pairs)  14 us
    all_to_all x2, starting transfers between devices, regroup(): lax.all_to_all(values, 'ord', 0, 0, axis_index_groups=groups, tiled=True)  12.4 us
    unnamed x28, local copies, waits for them, and re-layouts  7.42 us
    pallas_call x2, Pallas kernels, field_products(): pl.pallas_call(body, grid=(steps,), out_shape=jax.ShapeDtypeStruct((nlon,...  6.94 us
    dot_general x6, matrix products, level(): jnp.einsum('mcx,mhx->mch', there, level_interpolants[k, 1], preferred_ele...  4.75 us
  transfers between devices with their start and end apart: 18, of which 7 were waited for; matrix products, arithmetic and copies ran while one was open for 8% of the time, Pallas kernels for 5%

profile of v4, /device:TPU:1, one launch (start us, length us, event | category | flops | bytes accessed | tf_op | source)
XLA Modules:
  0.0 228.2 jit_solution(18377350015066521815)
XLA Ops:
  0.0 1.9 constant_dynamic-slice_fusion.1
  2.0 0.7 convolution_convert_fusion.1
  2.7 3.9 %collective-permute-start.3 = (bf16[8,256,128]{2,1,0:T(8,128)(2,1)S(1)}, bf16[8,256,128]{2,1,0:T(8,128)(2,1)}, u32[]{:S(2)}, u32[]{:S(2)}) collective-permute-start(bf16[8,256,128]{2,1,0:T(8,128)(2,1)S(1)} %convolution_convert_fusion.1), channel_id=1, source_target_pairs={{0,8},{1,9},{2,10},{3,11},{4,12},{5,13},{6,14},{7,15},{8,0},{9,1},... | collective-permute-start | bytes 1572872 | tf_op jit(solution)/shard_map/ppermute | solution.py:18
  6.6 0.9 slice.37
  7.5 5.1 %collective-permute-start.15 = (bf16[8,384,128]{2,1,0:T(8,128)(2,1)}, bf16[8,384,128]{2,1,0:T(8,128)(2,1)S(1)}, u32[]{:S(2)}, u32[]{:S(2)}) collective-permute-start(bf16[8,384,128]{2,1,0:T(8,128)(2,1)} %slice.37), channel_id=1, source_target_pairs={{0,32},{16,48},{32,0},{48,16},{64,96},{80,112},{96,64},{112,80},{1... | collective-permute-start | bytes 2359304 | tf_op jit(solution)/shard_map/ppermute | solution.py:18
  12.6 1.2 fusion.20
  13.9 48.8 %collective-permute-done.3 = bf16[8,256,128]{2,1,0:T(8,128)(2,1)} collective-permute-done((bf16[8,256,128]{2,1,0:T(8,128)(2,1)S(1)}, bf16[8,256,128]{2,1,0:T(8,128)(2,1)}, u32[]{:S(2)}, u32[]{:S(2)}) %collective-permute-start.3) | collective-permute-done | bytes 524320 | tf_op jit(solution)/shard_map/ppermute | solution.py:18
  62.6 1.4 fusion.3
  64.1 1.8 collective-permute-start.4
  65.8 1.8 constant_dynamic-slice_fusion
  68.0 8.6 %collective-permute-done.4 = bf16[8,256,128]{2,1,0:T(8,128)(2,1)S(1)} collective-permute-done((bf16[8,256,128]{2,1,0:T(8,128)(2,1)S(1)}, bf16[8,256,128]{2,1,0:T(8,128)(2,1)S(1)}, u32[]{:S(2)}, u32[]{:S(2)}) %collective-permute-start.4) | collective-permute-done | bytes 524320 | tf_op jit(solution)/shard_map/ppermute | solution.py:18
  76.9 3.4 %collective-permute-start.5 = (bf16[8,256,128]{2,1,0:T(8,128)(2,1)S(1)}, bf16[8,256,128]{2,1,0:T(8,128)(2,1)S(1)}, u32[]{:S(2)}, u32[]{:S(2)}) collective-permute-start(bf16[8,256,128]{2,1,0:T(8,128)(2,1)S(1)} %fusion.4), channel_id=1, source_target_pairs={{0,2},{1,3},{2,0},{3,1},{4,6},{5,7},{6,4},{7,5},{8,10},{9,11},{10,... | collective-permute-start | bytes 1572872 | tf_op jit(solution)/shard_map/ppermute | solution.py:18
  80.3 0.7 convolution_convert_fusion
  81.0 3.9 %collective-permute-start = (bf16[8,256,128]{2,1,0:T(8,128)(2,1)S(1)}, bf16[8,256,128]{2,1,0:T(8,128)(2,1)S(1)}, u32[]{:S(2)}, u32[]{:S(2)}) collective-permute-start(bf16[8,256,128]{2,1,0:T(8,128)(2,1)S(1)} %convolution_convert_fusion), channel_id=1, source_target_pairs={{0,8},{1,9},{2,10},{3,11},{4,12},{5,13},{6,14},{7,15},{8,0},{9,1},... | collective-permute-start | bytes 1572872 | tf_op jit(solution)/shard_map/ppermute | solution.py:18
  85.3 5.2 %collective-permute-done.5 = bf16[8,256,128]{2,1,0:T(8,128)(2,1)S(1)} collective-permute-done((bf16[8,256,128]{2,1,0:T(8,128)(2,1)S(1)}, bf16[8,256,128]{2,1,0:T(8,128)(2,1)S(1)}, u32[]{:S(2)}, u32[]{:S(2)}) %collective-permute-start.5) | collective-permute-done | bytes 524320 | tf_op jit(solution)/shard_map/ppermute | solution.py:18
  90.8 7.0 %collective-permute-start.6 = (bf16[8,256,128]{2,1,0:T(8,128)(2,1)S(1)}, bf16[8,256,128]{2,1,0:T(8,128)(2,1)S(1)}, u32[]{:S(2)}, u32[]{:S(2)}) collective-permute-start(bf16[8,256,128]{2,1,0:T(8,128)(2,1)S(1)} %fusion.5), channel_id=1, source_target_pairs={{0,32},{16,48},{32,0},{48,16},{64,96},{80,112},{96,64},{112,80},{1... | collective-permute-start | bytes 1572872 | tf_op jit(solution)/shard_map/ppermute | solution.py:18
  98.1 32.1 %collective-permute-done = bf16[8,256,128]{2,1,0:T(8,128)(2,1)S(1)} collective-permute-done((bf16[8,256,128]{2,1,0:T(8,128)(2,1)S(1)}, bf16[8,256,128]{2,1,0:T(8,128)(2,1)S(1)}, u32[]{:S(2)}, u32[]{:S(2)}) %collective-permute-start) | collective-permute-done | bytes 524320 | tf_op jit(solution)/shard_map/ppermute | solution.py:18
  130.2 1.1 fusion
  131.3 1.1 collective-permute-start.1
  132.4 0.9 copy-done.5
  133.3 1.1 copy-done.6
  134.5 1.4 latitude_values.3
  135.9 1.2 copy-done.2
  137.1 5.3 %all-to-all-start.1 = ((bf16[8,16,16,384]{3,2,1,0:T(8,128)(2,1)}), bf16[8,16,16,384]{3,2,1,0:T(8,128)(2,1)S(1)}, u32[]{:S(2)}, u32[]{:S(2)}) async-start(bf16[8,16,16,384]{3,2,1,0:T(8,128)(2,1)} %bitcast.84), calls=%async_computation.1 | async-start | bytes 3145728 | tf_op jit(solution)/shard_map/all_to_all | solution.py:203
  142.4 1.5 fusion.16
  144.0 1.3 fusion.1
  146.0 12.7 %collective-permute-done.2 = bf16[8,256,128]{2,1,0:T(8,128)(2,1)S(1)} collective-permute-done((bf16[8,256,128]{2,1,0:T(8,128)(2,1)S(1)}, bf16[8,256,128]{2,1,0:T(8,128)(2,1)S(1)}, u32[]{:S(2)}, u32[]{:S(2)}) %collective-permute-start.2) | collective-permute-done | bytes 524320 | tf_op jit(solution)/shard_map/ppermute | solution.py:18
  159.0 2.3 latitude_values.2
  161.2 1.5 copy-done.1
  163.0 7.1 %all-to-all-start = ((bf16[8,16,16,640]{3,2,1,0:T(8,128)(2,1)}), bf16[8,16,16,640]{3,2,1,0:T(8,128)(2,1)}, u32[]{:S(2)}, u32[]{:S(2)}) async-start(bf16[8,16,16,640]{3,2,1,0:T(8,128)(2,1)} %bitcast.83), calls=%async_computation | async-start | bytes 5242880 | tf_op jit(solution)/shard_map/all_to_all | solution.py:203
  170.1 1.9 slice.36
  172.0 6.8 %collective-permute-start.7 = (bf16[8,256,128]{2,1,0:T(8,128)(2,1)}, bf16[8,256,128]{2,1,0:T(8,128)(2,1)}, u32[]{:S(2)}, u32[]{:S(2)}) collective-permute-start(bf16[8,256,128]{2,1,0:T(8,128)(2,1)} %slice.36), channel_id=1, source_target_pairs={{0,32},{16,48},{32,0},{48,16},{64,96},{80,112},{96,64},{112,80},{1... | collective-permute-start | bytes 1572872 | tf_op jit(solution)/shard_map/ppermute | solution.py:18
  179.7 18.1 %collective-permute-done.7.factor_ref = bf16[8,256,128]{2,1,0:T(8,128)(2,1)} collective-permute-done((bf16[8,256,128]{2,1,0:T(8,128)(2,1)}, bf16[8,256,128]{2,1,0:T(8,128)(2,1)}, u32[]{:S(2)}, u32[]{:S(2)}) %collective-permute-start.7) | collective-permute-done | bytes 524320 | tf_op jit(solution)/shard_map/ppermute | solution.py:18
  197.8 2.9 %split_values.1 = (bf16[16,16,256]{2,1,0:T(8,128)(2,1)}, bf16[16,16,256]{2,1,0:T(8,128)(2,1)}, bf16[16,16,256]{2,1,0:T(8,128)(2,1)}, bf16[16,16,256]{2,1,0:T(8,1...) custom-call(s32[8]{0:T(128)S(1)} %stack.72.order_ref, ...), custom_call_target="tpu_custom_call" | custom-call | flops 134217728 | bytes 1048576 | tf_op jit(solution)/shard_map/split_values/pallas_call | solution.py:97
  200.7 0.6 copy-done.7
  201.3 0.7 copy-done.8
  202.0 0.6 copy-done.9
  203.3 2.7 %collective-permute-start.8 = (bf16[16,16,256]{2,1,0:T(8,128)(2,1)}, bf16[16,16,256]{2,1,0:T(8,128)(2,1)S(1)}, u32[]{:S(2)}, u32[]{:S(2)}) collective-permute-start(bf16[16,16,256]{2,1,0:T(8,128)(2,1)} %get-tuple-element.15), channel_id=1, source_target_pairs={{0,128},{16,144},{32,160},{48,176},{64,192},{80,208},{96,224},{112... | collective-permute-start | bytes 393224 | tf_op jit(solution)/shard_map/ppermute | solution.py:229
  206.0 5.1 %collective-permute-start.9 = (bf16[16,16,256]{2,1,0:T(8,128)(2,1)}, bf16[16,16,256]{2,1,0:T(8,128)(2,1)S(1)}, u32[]{:S(2)}, u32[]{:S(2)}) collective-permute-start(bf16[16,16,256]{2,1,0:T(8,128)(2,1)} %get-tuple-element.16), channel_id=1, source_target_pairs={{0,144},{16,128},{32,176},{48,160},{64,208},{80,192},{96,240},{112... | collective-permute-start | bytes 393224 | tf_op jit(solution)/shard_map/ppermute | solution.py:229
  211.2 0.7 copy.16
  212.6 0.7 copy.17
  213.3 0.7 copy.21
  214.0 1.4 collective-permute-start.10
  215.4 1.3 collective-permute-start.11
  216.7 3.0 %collective-permute-start.13 = (bf16[16,16,256]{2,1,0:T(8,128)(2,1)}, bf16[16,16,256]{2,1,0:T(8,128)(2,1)}, u32[]{:S(2)}, u32[]{:S(2)}) collective-permute-start(bf16[16,16,256]{2,1,0:T(8,128)(2,1)} %copy-done.8), channel_id=1, source_target_pairs={{0,208},{16,192},{32,240},{48,224},{64,16},{80,0},{96,48},{112,32}... | collective-permute-start | bytes 393224 | tf_op jit(solution)/shard_map/ppermute | solution.py:229
  220.2 0.9 fusion.37
  221.2 4.1 %field_products.2.refs_8_ = bf16[256,8,640]{2,1,0:T(8,128)(2,1)} custom-call(bf16[256,256]{1,0:T(8,128)(2,1)S(1)} %get-tuple-element.25.table_ref, bf16[8,16,16,640]{3,2,1,0:T(8,128)(2,1)} %all-to-all-done.near_ref, bf16[8,16,16,384]{3,2,1,0:T(8,128)(2,1)S(1)} %all-to-all-done.1.refs_0_), custom_call_target="tpu_custom_call" | custom-call | flops 805306368 | bytes 4718592 | tf_op jit(solution)/shard_map/field_products/pallas_call | solution.py:147
  225.3 2.9 %field_products.3 = bf16[256,8,640]{2,1,0:T(8,128)(2,1)} custom-call(bf16[256,256]{1,0:T(8,128)(2,1)S(1)} %get-tuple-element.26.table_ref, bf16[8,16,16,640]{3,2,1,0:T(8,128)(2,1)} %all-to-all-done.near_ref, bf16[1,16,16,256]{3,2,1,0:T(8,128)(2,1)S(1)} %bitcast.86, bf16[1,16,16,256]{3,2,1,0:T(8,128)(2,1)S(1)} %bitcast.87, ...), custom_call_target="tpu_custom_call", output_to_operand_aliasing={{}: (10, {})} | custom-call | flops 536870912 | bytes 3145728 | tf_op jit(solution)/shard_map/field_products/pallas_call | solution.py:147
  (53 shorter events, 5.6 us)
Async XLA Ops:
  0.0 1.9 copy-start
  1.9 4.6 %copy-start.3 = (bf16[8,640,128]{2,1,0:T(8,128)(2,1)S(1)}, bf16[8,640,128]{2,1,0:T(8,128)(2,1)}, u32[]{:S(2)}) copy-start(bf16[8,640,128]{2,1,0:T(8,128)(2,1)} %refs_0_.1) | copy-start | bytes 3932164
  2.7 60.0 %collective-permute-start.3 = (bf16[8,256,128]{2,1,0:T(8,128)(2,1)S(1)}, bf16[8,256,128]{2,1,0:T(8,128)(2,1)}, u32[]{:S(2)}, u32[]{:S(2)}) collective-permute-start(bf16[8,256,128]{2,1,0:T(8,128)(2,1)S(1)} %convolution_convert_fusion.1), channel_id=1, source_target_pairs={{0,8},{1,9},{2,10},{3,11},{4,12},{5,13},{6,14},{7,15},{8,0},{9,1},... | collective-permute-start | bytes 1572872 | tf_op jit(solution)/shard_map/ppermute | solution.py:18
  7.5 124.9 %collective-permute-start.15 = (bf16[8,384,128]{2,1,0:T(8,128)(2,1)}, bf16[8,384,128]{2,1,0:T(8,128)(2,1)S(1)}, u32[]{:S(2)}, u32[]{:S(2)}) collective-permute-start(bf16[8,384,128]{2,1,0:T(8,128)(2,1)} %slice.37), channel_id=1, source_target_pairs={{0,32},{16,48},{32,0},{48,16},{64,96},{80,112},{96,64},{112,80},{1... | collective-permute-start | bytes 2359304 | tf_op jit(solution)/shard_map/ppermute | solution.py:18
  64.1 3.6 %copy-start.11 = (bf16[3,2,8,128,128]{4,3,2,1,0:T(8,128)(2,1)S(1)}, bf16[3,2,8,128,128]{4,3,2,1,0:T(8,128)(2,1)}, u32[]{:S(2)}) copy-start(bf16[3,2,8,128,128]{4,3,2,1,0:T(8,128)(2,1)} %param.7) | copy-start | bytes 4718596
  64.1 12.6 %collective-permute-start.4 = (bf16[8,256,128]{2,1,0:T(8,128)(2,1)S(1)}, bf16[8,256,128]{2,1,0:T(8,128)(2,1)S(1)}, u32[]{:S(2)}, u32[]{:S(2)}) collective-permute-start(bf16[8,256,128]{2,1,0:T(8,128)(2,1)S(1)} %fusion.3), channel_id=1, source_target_pairs={{0,4},{1,5},{2,6},{3,7},{4,0},{5,1},{6,2},{7,3},{8,12},{9,13},{10,... | collective-permute-start | bytes 1572872 | tf_op jit(solution)/shard_map/ppermute | solution.py:18
  76.9 13.6 %collective-permute-start.5 = (bf16[8,256,128]{2,1,0:T(8,128)(2,1)S(1)}, bf16[8,256,128]{2,1,0:T(8,128)(2,1)S(1)}, u32[]{:S(2)}, u32[]{:S(2)}) collective-permute-start(bf16[8,256,128]{2,1,0:T(8,128)(2,1)S(1)} %fusion.4), channel_id=1, source_target_pairs={{0,2},{1,3},{2,0},{3,1},{4,6},{5,7},{6,4},{7,5},{8,10},{9,11},{10,... | collective-permute-start | bytes 1572872 | tf_op jit(solution)/shard_map/ppermute | solution.py:18
  81.0 49.2 %collective-permute-start = (bf16[8,256,128]{2,1,0:T(8,128)(2,1)S(1)}, bf16[8,256,128]{2,1,0:T(8,128)(2,1)S(1)}, u32[]{:S(2)}, u32[]{:S(2)}) collective-permute-start(bf16[8,256,128]{2,1,0:T(8,128)(2,1)S(1)} %convolution_convert_fusion), channel_id=1, source_target_pairs={{0,8},{1,9},{2,10},{3,11},{4,12},{5,13},{6,14},{7,15},{8,0},{9,1},... | collective-permute-start | bytes 1572872 | tf_op jit(solution)/shard_map/ppermute | solution.py:18
  90.8 42.5 %collective-permute-start.6 = (bf16[8,256,128]{2,1,0:T(8,128)(2,1)S(1)}, bf16[8,256,128]{2,1,0:T(8,128)(2,1)S(1)}, u32[]{:S(2)}, u32[]{:S(2)}) collective-permute-start(bf16[8,256,128]{2,1,0:T(8,128)(2,1)S(1)} %fusion.5), channel_id=1, source_target_pairs={{0,32},{16,48},{32,0},{48,16},{64,96},{80,112},{96,64},{112,80},{1... | collective-permute-start | bytes 1572872 | tf_op jit(solution)/shard_map/ppermute | solution.py:18
  131.3 12.6 %collective-permute-start.1 = (bf16[8,256,128]{2,1,0:T(8,128)(2,1)}, bf16[8,256,128]{2,1,0:T(8,128)(2,1)}, u32[]{:S(2)}, u32[]{:S(2)}) collective-permute-start(bf16[8,256,128]{2,1,0:T(8,128)(2,1)} %fusion), channel_id=1, source_target_pairs={{0,4},{1,5},{2,6},{3,7},{4,0},{5,1},{6,2},{7,3},{8,12},{9,13},{10,... | collective-permute-start | bytes 1572872 | tf_op jit(solution)/shard_map/ppermute | solution.py:18
  132.4 0.9 copy-start.5
  133.3 1.1 copy-start.6
  135.9 1.2 copy-start.2
  137.1 25.9 %all-to-all-start.1 = ((bf16[8,16,16,384]{3,2,1,0:T(8,128)(2,1)}), bf16[8,16,16,384]{3,2,1,0:T(8,128)(2,1)S(1)}, u32[]{:S(2)}, u32[]{:S(2)}) async-start(bf16[8,16,16,384]{3,2,1,0:T(8,128)(2,1)} %bitcast.84), calls=%async_computation.1 | async-start | bytes 3145728 | tf_op jit(solution)/shard_map/all_to_all | solution.py:203
  142.4 1.6 copy-start.12
  145.4 13.3 %collective-permute-start.2 = (bf16[8,256,128]{2,1,0:T(8,128)(2,1)S(1)}, bf16[8,256,128]{2,1,0:T(8,128)(2,1)S(1)}, u32[]{:S(2)}, u32[]{:S(2)}) collective-permute-start(bf16[8,256,128]{2,1,0:T(8,128)(2,1)S(1)} %fusion.1), channel_id=1, source_target_pairs={{0,2},{1,3},{2,0},{3,1},{4,6},{5,7},{6,4},{7,5},{8,10},{9,11},{10,... | collective-permute-start | bytes 1572872 | tf_op jit(solution)/shard_map/ppermute | solution.py:18
  146.0 13.0 %copy-start.4 = (bf16[8,640,128]{2,1,0:T(8,128)(2,1)S(1)}, bf16[8,640,128]{2,1,0:T(8,128)(2,1)}, u32[]{:S(2)}) copy-start(bf16[8,640,128]{2,1,0:T(8,128)(2,1)} %refs_0_.1) | copy-start | bytes 3932164
  161.2 1.5 copy-start.1
  163.0 15.8 %copy-start.13 = (s32[128]{0:T(128)S(1)}, s32[128]{0:T(128)}, u32[]{:S(2)}) copy-start(s32[128]{0:T(128)} %param.9) | copy-start | bytes 1540
  163.0 58.2 %all-to-all-start = ((bf16[8,16,16,640]{3,2,1,0:T(8,128)(2,1)}), bf16[8,16,16,640]{3,2,1,0:T(8,128)(2,1)}, u32[]{:S(2)}, u32[]{:S(2)}) async-start(bf16[8,16,16,640]{3,2,1,0:T(8,128)(2,1)} %bitcast.83), calls=%async_computation | async-start | bytes 5242880 | tf_op jit(solution)/shard_map/all_to_all | solution.py:203
  172.0 25.8 %collective-permute-start.7 = (bf16[8,256,128]{2,1,0:T(8,128)(2,1)}, bf16[8,256,128]{2,1,0:T(8,128)(2,1)}, u32[]{:S(2)}, u32[]{:S(2)}) collective-permute-start(bf16[8,256,128]{2,1,0:T(8,128)(2,1)} %slice.36), channel_id=1, source_target_pairs={{0,32},{16,48},{32,0},{48,16},{64,96},{80,112},{96,64},{112,80},{1... | collective-permute-start | bytes 1572872 | tf_op jit(solution)/shard_map/ppermute | solution.py:18
  200.7 0.6 copy-start.7
  201.3 0.7 copy-start.8
  202.0 0.6 copy-start.9
  202.6 0.6 copy-start.10
  203.3 13.4 %collective-permute-start.8 = (bf16[16,16,256]{2,1,0:T(8,128)(2,1)}, bf16[16,16,256]{2,1,0:T(8,128)(2,1)S(1)}, u32[]{:S(2)}, u32[]{:S(2)}) collective-permute-start(bf16[16,16,256]{2,1,0:T(8,128)(2,1)} %get-tuple-element.15), channel_id=1, source_target_pairs={{0,128},{16,144},{32,160},{48,176},{64,192},{80,208},{96,224},{112... | collective-permute-start | bytes 393224 | tf_op jit(solution)/shard_map/ppermute | solution.py:229
  206.0 13.7 %collective-permute-start.9 = (bf16[16,16,256]{2,1,0:T(8,128)(2,1)}, bf16[16,16,256]{2,1,0:T(8,128)(2,1)S(1)}, u32[]{:S(2)}, u32[]{:S(2)}) collective-permute-start(bf16[16,16,256]{2,1,0:T(8,128)(2,1)} %get-tuple-element.16), channel_id=1, source_target_pairs={{0,144},{16,128},{32,176},{48,160},{64,208},{80,192},{96,240},{112... | collective-permute-start | bytes 393224 | tf_op jit(solution)/shard_map/ppermute | solution.py:229
  214.0 11.2 %collective-permute-start.10 = (bf16[16,16,256]{2,1,0:T(8,128)(2,1)}, bf16[16,16,256]{2,1,0:T(8,128)(2,1)S(1)}, u32[]{:S(2)}, u32[]{:S(2)}) collective-permute-start(bf16[16,16,256]{2,1,0:T(8,128)(2,1)} %get-tuple-element.17), channel_id=1, source_target_pairs={{0,64},{16,80},{32,96},{48,112},{64,128},{80,144},{96,160},{112,17... | collective-permute-start | bytes 393224 | tf_op jit(solution)/shard_map/ppermute | solution.py:229
  215.4 9.9 %collective-permute-start.11 = (bf16[16,16,256]{2,1,0:T(8,128)(2,1)}, bf16[16,16,256]{2,1,0:T(8,128)(2,1)S(1)}, u32[]{:S(2)}, u32[]{:S(2)}) collective-permute-start(bf16[16,16,256]{2,1,0:T(8,128)(2,1)} %copy-done.10), channel_id=1, source_target_pairs={{0,192},{16,208},{32,224},{48,240},{64,0},{80,16},{96,32},{112,48}... | collective-permute-start | bytes 393224 | tf_op jit(solution)/shard_map/ppermute | solution.py:229
  216.7 8.6 %collective-permute-start.12 = (bf16[16,16,256]{2,1,0:T(8,128)(2,1)}, bf16[16,16,256]{2,1,0:T(8,128)(2,1)}, u32[]{:S(2)}, u32[]{:S(2)}) collective-permute-start(bf16[16,16,256]{2,1,0:T(8,128)(2,1)} %copy-done.9), channel_id=1, source_target_pairs={{0,80},{16,64},{32,112},{48,96},{64,144},{80,128},{96,176},{112,16... | collective-permute-start | bytes 393224 | tf_op jit(solution)/shard_map/ppermute | solution.py:229
  216.7 8.6 %collective-permute-start.13 = (bf16[16,16,256]{2,1,0:T(8,128)(2,1)}, bf16[16,16,256]{2,1,0:T(8,128)(2,1)}, u32[]{:S(2)}, u32[]{:S(2)}) collective-permute-start(bf16[16,16,256]{2,1,0:T(8,128)(2,1)} %copy-done.8), channel_id=1, source_target_pairs={{0,208},{16,192},{32,240},{48,224},{64,16},{80,0},{96,48},{112,32}... | collective-permute-start | bytes 393224 | tf_op jit(solution)/shard_map/ppermute | solution.py:229
  219.7 5.6 %collective-permute-start.14 = (bf16[16,16,256]{2,1,0:T(8,128)(2,1)}, bf16[16,16,256]{2,1,0:T(8,128)(2,1)}, u32[]{:S(2)}, u32[]{:S(2)}) collective-permute-start(bf16[16,16,256]{2,1,0:T(8,128)(2,1)} %copy-done.7), channel_id=1, source_target_pairs={{0,16},{16,0},{32,48},{48,32},{64,80},{80,64},{96,112},{112,96},{1... | collective-permute-start | bytes 393224 | tf_op jit(solution)/shard_map/ppermute | solution.py:229
